TPU v7x, 32 devices: a whole 2x2x4 slice. The times are simulated.
32 devices in a mesh: lon: 4 (over z), lat: 8 (over y, x, core).
Axes of the slice: x: 2, y: 2, z: 4, core: 2. Of those that a mesh axis runs over, the one named last changes fastest.
Arguments:
- fields: float32 [4, 8, 512, 3600], P(None, None, 'lat', 'lon'), may hold values from -6 to 6
- thickness: float32 [8], replicated, may hold values from 5 to 250
- cutoff: int32 [256], replicated, may hold values from 2 to 1800
- barotropic: float32 [3, 512, 3600], P(None, 'lat', 'lon'), may hold values from -6 to 6
- land_sea: int32 [512, 3600], P('lat', 'lon'), may hold values 0 or 1
Outputs:
- filtered_tracers: float32 [2, 8, 512, 3600], P(None, None, 'lat', 'lon')
- velocity: float32 [2, 8, 512, 3600], P(None, None, 'lat', 'lon')
- sea_level: float32 [512, 3600], P('lat', 'lon')
Inputs may be any that keep to these rules, and one draw needn't show every extreme that they name: `cutoff`: each filtered row's highest kept wavenumber.
All inputs are finite; a program needn't handle non-finite values. No bound on the sum of `land_sea` on one device may be relied on, other than what follows from the above.
Results may differ from a plain program's by a relative error of at most 0.0003.
Values sent between devices are 32-bit elements; how exact they have to be, the bound alone decides.
A program may use at most 128 MiB of HBM per device.

v0:
```python
import math

import jax
import jax.numpy as jnp
from jax import lax
from jax.sharding import PartitionSpec as P

POLE_DEV = 2
SUB = 20


wave_coef = 0.65
highest = lax.Precision.HIGHEST


def with_halo(value, sides, width):
    for axis, dim in sides:
        devices, length = (lax.axis_size(axis), value.shape[dim])
        up = [(i, (i + 1) % devices) for i in range(devices)]
        down = [(j, i) for i, j in up]
        last = lax.slice_in_dim(value, length - width, length, axis=dim)
        initial = lax.slice_in_dim(value, 0, width, axis=dim)
        before = lax.ppermute(last, axis, up)
        after = lax.ppermute(initial, axis, down)
        value = jnp.concatenate([before, value, after], axis=dim)
    return value


def trig_tables(rows_len, cols_len, period):
    product = lax.broadcasted_iota(jnp.int32, (rows_len, cols_len), 0) * lax.broadcasted_iota(
        jnp.int32, (rows_len, cols_len), 1
    )
    angles = (product % period).astype(jnp.float32) * (2.0 * math.pi / period)
    return (jnp.cos(angles), jnp.sin(angles))


def spectral_cut(values, row_cuts):
    item_count, circle_len = values.shape
    first_len = max((d for d in range(1, math.isqrt(circle_len) + 1) if circle_len % d == 0))
    second_len = circle_len // first_len
    cos_first, sin_first = trig_tables(first_len, first_len, first_len)
    cos_second, sin_second = trig_tables(second_len, second_len, second_len)
    twist_cos, twist_sin = trig_tables(first_len, second_len, circle_len)
    grid = values.reshape(item_count, first_len, second_len)
    step_real = jnp.einsum("inb,nm->imb", grid, cos_first, precision=highest)
    step_imag = -jnp.einsum("inb,nm->imb", grid, sin_first, precision=highest)
    turn_real = step_real * twist_cos + step_imag * twist_sin
    turn_imag = step_imag * twist_cos - step_real * twist_sin
    spec_real = jnp.einsum("imb,bk->imk", turn_real, cos_second, precision=highest) + jnp.einsum(
        "imb,bk->imk", turn_imag, sin_second, precision=highest
    )
    spec_imag = jnp.einsum("imb,bk->imk", turn_imag, cos_second, precision=highest) - jnp.einsum(
        "imb,bk->imk", turn_real, sin_second, precision=highest
    )
    wavenumber = lax.broadcasted_iota(
        jnp.int32, (first_len, second_len), 0
    ) + first_len * lax.broadcasted_iota(jnp.int32, (first_len, second_len), 1)
    folded = jnp.minimum(wavenumber, circle_len - wavenumber)
    kept_mask = jnp.where(folded[None, :, :] <= row_cuts[:, None, None], 1.0 / circle_len, 0.0)
    spec_real = spec_real * kept_mask
    spec_imag = spec_imag * kept_mask
    part_real = jnp.einsum("imq,qk->imk", spec_real, cos_second, precision=highest) - jnp.einsum(
        "imq,qk->imk", spec_imag, sin_second, precision=highest
    )
    part_imag = jnp.einsum("imq,qk->imk", spec_real, sin_second, precision=highest) + jnp.einsum(
        "imq,qk->imk", spec_imag, cos_second, precision=highest
    )
    back_real = part_real * twist_cos - part_imag * twist_sin
    back_imag = part_real * twist_sin + part_imag * twist_cos
    rebuilt = jnp.einsum("imk,mj->ijk", back_real, cos_first, precision=highest) - jnp.einsum(
        "imk,mj->ijk", back_imag, sin_first, precision=highest
    )
    return rebuilt.reshape(item_count, circle_len)


def row_cutoffs(cutoff, band, item_ids, band_rows, total_rows):
    pole_rows = cutoff.shape[0] // 2
    global_row = band * band_rows + item_ids % band_rows
    table_index = jnp.where(
        global_row < pole_rows, global_row, global_row - (total_rows - 2 * pole_rows)
    )
    matches = table_index[:, None] == lax.broadcasted_iota(jnp.int32, (1, 2 * pole_rows), 1)
    return jnp.sum(jnp.where(matches, cutoff[None, :], 0), axis=1)


def body(fields, thickness, cutoff, barotropic, land_sea):
    lon_count = lax.axis_size("lon")
    lat_count = lax.axis_size("lat")
    lat_index = lax.axis_index("lat")
    lon_index = lax.axis_index("lon")
    components, levels, band_rows, tile_cols = fields.shape
    total_rows = band_rows * lat_count
    total_items = components * levels * band_rows
    share_items = total_items // lon_count
    flattened = fields.reshape(total_items, tile_cols)
    circled = lax.all_to_all(flattened, "lon", split_axis=0, concat_axis=1, tiled=True)
    item_ids = lon_index * share_items + lax.iota(jnp.int32, share_items)
    north_pole = lat_index < POLE_DEV
    south_pole = lat_index >= lat_count - POLE_DEV
    row_cuts = row_cutoffs(cutoff, lat_index, item_ids, band_rows, total_rows)
    result = lax.cond(
        north_pole | south_pole,
        lambda values: spectral_cut(values, row_cuts),
        lambda values: values,
        circled,
    )
    returned = lax.all_to_all(result, "lon", split_axis=1, concat_axis=0, tiled=True)
    filtered = returned.reshape(components, levels, band_rows, tile_cols)
    rim_width = 4
    mask_wide = with_halo(land_sea, (("lon", 1), ("lat", 0)), rim_width + 1)
    ocean_wide = mask_wide.astype(jnp.float32)
    pad_rows = (
        lat_index * band_rows - rim_width - 1 + lax.iota(jnp.int32, band_rows + 2 * rim_width + 2)
    ) % total_rows
    east_wide = ocean_wide * jnp.roll(ocean_wide, -1, 1)
    north_wide = (
        ocean_wide
        * jnp.roll(ocean_wide, -1, 0)
        * (pad_rows != total_rows - 1).astype(jnp.float32)[:, None]
    )
    ocean_pad = ocean_wide[1:-1, 1:-1]
    east_pad = east_wide[1:-1, 1:-1]
    north_pad = north_wide[1:-1, 1:-1]

    def advance(cycle_index, state_now):
        padded = with_halo(state_now, (("lon", 2), ("lat", 1)), rim_width)
        surface = padded[0]
        eastward = padded[1] * east_pad
        northward = padded[2] * north_pad
        for subcycle in range(rim_width):
            divergence = eastward - jnp.roll(eastward, 1, 1) + northward - jnp.roll(northward, 1, 0)
            surface = surface - wave_coef * ocean_pad * divergence
            eastward = east_pad * (eastward - wave_coef * (jnp.roll(surface, -1, 1) - surface))
            northward = north_pad * (northward - wave_coef * (jnp.roll(surface, -1, 0) - surface))
        return jnp.stack([surface, eastward, northward])[
            :, rim_width:-rim_width, rim_width:-rim_width
        ]

    final_state = lax.fori_loop(0, SUB // rim_width, advance, barotropic)
    east_mid = east_pad[rim_width:-rim_width, rim_width:-rim_width]
    north_mid = north_pad[rim_width:-rim_width, rim_width:-rim_width]
    weights = thickness / jnp.sum(thickness)
    currents = filtered[2:]
    column = jnp.einsum("k,ckij->cij", weights, currents, precision=highest)
    velocity = jnp.stack([east_mid, north_mid])[:, None] * (
        currents - column[:, None] + final_state[1:][:, None]
    )
    return (filtered[:2], velocity, final_state[0])


def solution(mesh):
    return jax.shard_map(
        body,
        mesh=mesh,
        in_specs=(P(None, None, "lat", "lon"), P(), P(), P(None, "lat", "lon"), P("lat", "lon")),
        out_specs=(P(None, None, "lat", "lon"), P(None, None, "lat", "lon"), P("lat", "lon")),
        check_vma=False,
    )
```

profile of v0, /device:TPU:0, one launch (start us, length us, event | category | flops | bytes accessed | tf_op | source)
XLA Modules:
  0.0 685.9 jit_solution(6149009317517989058)
XLA Ops:
  0.6 8.5 %copy.117 = f32[4,512,900]{1,2,0:T(8,128)} copy(f32[4,512,900]{2,1,0:T(8,128)} %bitcast.266) | data formatting | bytes 14745600 | tf_op jit(solution)/shard_map/all_to_all | solution.py:96
  9.2 6.5 all-to-all-start
  15.7 4.2 collective-permute-start.5
  19.9 116.0 %collective-permute-done.5 = s32[64,5]{1,0:T(8,128)S(1)} collective-permute-done((s32[64,5]{1,0:T(8,128)S(1)}, s32[64,5]{1,0:T(8,128)S(1)}, u32[]{:S(2)}, u32[]{:S(2)}) %collective-permute-start.5) | collective-permute-done | bytes 1312 | tf_op jit(solution)/shard_map/ppermute | solution.py:24
  135.9 5.3 collective-permute-done.4
  141.3 0.9 collective-permute-start.7
  142.8 1.0 collective-permute-done.7
  143.9 2.6 collective-permute-done.6
  148.1 31.4 %all-to-all-done = f32[4,512,900]{1,2,0:T(8,128)} async-done(((f32[4,512,900]{1,2,0:T(8,128)}), f32[4,512,900]{1,2,0:T(8,128)}, u32[]{:S(2)}, u32[]{:S(2)}) %all-to-all-start) | async-done | bytes 7372832 | tf_op jit(solution)/shard_map/all_to_all | solution.py:96
  179.6 5.4 all_to_all.32
  185.0 209.4 %conditional.1 = (f32[512,3600]{0,1:T(8,128)}) conditional(s32[]{:T(128)} %convert_element_type.71, f32[512,3600]{0,1:T(8,128)} %all_to_all.32, (f32[512,3600]{0,1:T(8,128)}, s32[]{:T(128)}, s32[]{:T(128)}, s32[512,1]{0,1:T(1,128)S(1)}, s32[]{:T(128)}, /*index=5*/s32[512,256]{1,0:T(8,128)S(1)}, s32[256]{0:T(256)S(1)}, s32[]{:T(128)}) %tuple.174), branch_computations={%region_0.1_spmd, %region_1.3_spmd.clone} | conditional | flops 15970319360 | bytes 406258240 | solution.py:101
  185.3 7.7 %reshape.238 = f32[512,60,60]{0,2,1:T(8,128)} reshape(f32[512,3600]{0,1:T(8,128)} %get-tuple-element.189) | data formatting | bytes 14745600 | tf_op jit(solution)/shard_map/cond/branch_1_fun/reshape | solution.py:44
  193.0 16.4 %fusion.86 = f32[60,512,60]{1,0,2:T(8,128)} fusion(f32[512,60,60]{0,2,1:T(8,128)} %reshape.238), kind=kOutput, calls=%fused_computation.157 | convolution fusion | flops 1327136384 | bytes 14745600 | tf_op jit(solution)/shard_map/cond/branch_1_fun/inb,nm->imb/dot_general | solution.py:46
  209.5 19.7 %add_bitcast_fusion = (f32[512,60,60]{0,1,2:T(8,128)}, f32[512,60,60]{0,1,2:T(8,128)S(1)}) fusion(f32[60,512,60]{1,0,2:T(8,128)} %fusion.86, f32[60,60]{0,1:T(8,128)S(1)} %get-tuple-element.247, f32[60,60]{0,1:T(8,128)S(1)} %get-tuple-element.248, f32[512,60,60]{0,2,1:T(8,128)} %reshape.238), kind=kOutput, calls=%fused_computation.148 | convolution fusion | flops 1340038784 | bytes 29520000 | tf_op jit(solution)/shard_map/cond/branch_1_fun/inb,nm->imb/dot_general | solution.py:45
  229.2 13.1 %fusion.78 = f32[512,60,60]{0,2,1:T(8,128)} fusion(f32[512,60,60]{0,1,2:T(8,128)S(1)} %get-tuple-element.246), kind=kOutput, calls=%fused_computation.149 | convolution fusion | flops 1327136384 | bytes 14745600 | tf_op jit(solution)/shard_map/cond/branch_1_fun/imb,bk->imk/dot_general | solution.py:52
  242.7 20.5 %select_multiply_fusion = f32[512,60,60]{0,2,1:T(8,128)S(1)} fusion(f32[512,60,60]{0,2,1:T(8,128)} %fusion.78, s32[512]{0:T(512)S(1)} %select_reduce_fusion, s32[60,60]{1,0:T(8,128)S(1)} %copy.109, f32[512,60,60]{0,1,2:T(8,128)} %get-tuple-element.245), kind=kOutput, calls=%fused_computation.138 | convolution fusion | flops 1334509184 | bytes 22134848 | tf_op jit(solution)/shard_map/cond/branch_1_fun/imb,bk->imk/dot_general | solution.py:52
  263.2 10.0 %fusion.109 = f32[512,60,60]{0,2,1:T(8,128)} fusion(f32[512,60,60]{0,2,1:T(8,128)S(1)} %select_multiply_fusion), kind=kOutput, calls=%fused_computation.178 | convolution fusion | flops 1327136384 | bytes 14745600 | tf_op jit(solution)/shard_map/cond/branch_1_fun/imq,qk->imk/dot_general | solution.py:65
  273.2 13.1 %fusion.80 = f32[512,60,60]{0,2,1:T(8,128)} fusion(f32[512,60,60]{0,1,2:T(8,128)S(1)} %copy-done.3), kind=kOutput, calls=%fused_computation.151 | convolution fusion | flops 1327136384 | bytes 14745600 | tf_op jit(solution)/shard_map/cond/branch_1_fun/imb,bk->imk/dot_general | solution.py:49
  286.3 20.0 %select_multiply_fusion.1 = f32[512,60,60]{0,2,1:T(8,128)S(1)} fusion(f32[512,60,60]{0,2,1:T(8,128)} %fusion.80, s32[512]{0:T(512)S(1)} %select_reduce_fusion, s32[60,60]{1,0:T(8,128)S(1)} %copy.109, f32[512,60,60]{0,1,2:T(8,128)} %get-tuple-element.245), kind=kOutput, calls=%fused_computation.139 | convolution fusion | flops 1334509184 | bytes 22134848 | tf_op jit(solution)/shard_map/cond/branch_1_fun/imb,bk->imk/dot_general | solution.py:49
  306.3 3.1 copy-done.1
  309.4 9.8 %fusion.112 = f32[512,60,60]{0,2,1:T(8,128)} fusion(f32[512,60,60]{0,2,1:T(8,128)S(1)} %select_multiply_fusion.1), kind=kOutput, calls=%fused_computation.181 | convolution fusion | flops 1327136384 | bytes 14745600 | tf_op jit(solution)/shard_map/cond/branch_1_fun/imq,qk->imk/dot_general | solution.py:62
  319.2 10.2 %fusion.103 = f32[512,60,60]{0,2,1:T(8,128)} fusion(f32[512,60,60]{0,2,1:T(8,128)S(1)} %select_multiply_fusion), kind=kOutput, calls=%fused_computation.172 | convolution fusion | flops 1327136384 | bytes 14745600 | tf_op jit(solution)/shard_map/cond/branch_1_fun/imq,qk->imk/dot_general | solution.py:62
  329.3 22.0 %multiply_subtract_fusion = (f32[512,60,60]{0,2,1:T(8,128)}, f32[512,60,60]{0,2,1:T(8,128)}) fusion(f32[60,60]{1,0:T(8,128)S(1)} %copy.113, f32[60,60]{1,0:T(8,128)S(1)} %copy.112, f32[512,60,60]{0,2,1:T(8,128)} %fusion.109, f32[512,60,60]{0,2,1:T(8,128)} %fusion.112, f32[512,60,60]{0,2,1:T(8,128)} %fusion.103, f32[512,60,60]{0,2,1:T(8,128)} %copy-done.1), kind=kOutput, calls=%fused_computation.146 | convolution fusion | flops 1341881984 | bytes 44265600 | tf_op jit(solution)/shard_map/cond/branch_1_fun/imq,qk->imk/dot_general | solution.py:65
  351.3 15.7 %fusion.74 = f32[60,512,60]{1,0,2:T(8,128)S(1)} fusion(f32[512,60,60]{0,2,1:T(8,128)} %get-tuple-element.244), kind=kOutput, calls=%fused_computation.140 | convolution fusion | flops 1327136384 | bytes 14745600 | tf_op jit(solution)/shard_map/cond/branch_1_fun/imk,mj->ijk/dot_general | solution.py:70
  367.0 11.8 %subtract_bitcast_fusion = f32[512,60,60]{0,1,2:T(8,128)S(1)} fusion(f32[60,512,60]{1,0,2:T(8,128)S(1)} %fusion.74, f32[512,60,60]{0,2,1:T(8,128)S(1)} %copy-done.5), kind=kOutput, calls=%fused_computation.144 | convolution fusion | flops 1328979584 | bytes 22118400 | tf_op jit(solution)/shard_map/cond/branch_1_fun/imk,mj->ijk/dot_general | solution.py:70
  378.8 7.6 %copy.116 = f32[512,60,60]{0,2,1:T(8,128)} copy(f32[512,60,60]{0,1,2:T(8,128)S(1)} %subtract_bitcast_fusion) | data formatting | bytes 14745600 | tf_op jit(solution)/shard_map/cond/branch_1_fun/sub | solution.py:70
  386.5 7.6 %reshape.239 = f32[512,3600]{0,1:T(8,128)} reshape(f32[512,60,60]{0,2,1:T(8,128)} %copy.116) | data formatting | bytes 14745600 | tf_op jit(solution)/shard_map/cond/branch_1_fun/reshape | solution.py:73
  394.3 5.4 all_to_all.33
  399.8 9.1 %all-to-all-start.1 = ((f32[512,4,900]{0,2,1:T(8,128)}), f32[512,4,900]{0,2,1:T(8,128)}, u32[]{:S(2)}, u32[]{:S(2)}) async-start(f32[512,4,900]{0,2,1:T(8,128)} %all_to_all.33), calls=%async_computation.1 | async-start | bytes 14811136 | tf_op jit(solution)/shard_map/all_to_all | solution.py:107
  408.9 246.6 %while.10 = (s32[]{:T(128)}, f32[3,64,900]{2,1,0:T(8,128)S(1)}, f32[72,908]{1,0:T(8,128)S(1)}, f32[72,908]{1,0:T(8,128)S(1)}, f32[72,908]{1,0:T(8,128)S(1)}, /*index=5*/s32[]{:T(128)}) while((s32[]{:T(128)}, f32[3,64,900]{2,1,0:T(8,128)S(1)}, f32[72,908]{1,0:T(8,128)S(1)}, f32[72,908]{1,0:T(8,128)S(1)}, f32[72,908]{1,0:T(8,128)S(1)}, ...), condition=%wide.region_5.6_spmd, body=%wide.region_4.5_spmd.sunk | while | flops 10783970 | bytes 43440612 | solution.py:139
  408.9 3.9 collective-permute-start
  413.3 116.4 %collective-permute-done = f32[3,64,4]{2,1,0:T(8,128)S(1)} collective-permute-done((f32[3,64,4]{2,1,0:T(8,128)S(1)}, f32[3,64,4]{2,1,0:T(8,128)S(1)}, u32[]{:S(2)}, u32[]{:S(2)}) %collective-permute-start) | collective-permute-done | bytes 3104 | tf_op jit(solution)/shard_map/while/body/eval_jaxpr/ppermute | solution.py:24
  529.6 5.2 collective-permute-done.1
  535.5 1.4 collective-permute-done.2
  536.9 3.0 collective-permute-done.3
  543.9 0.6 fusion.257
  545.0 42.7 %collective-permute-start.1 = (f32[3,64,4]{2,1,0:T(8,128)S(1)}, f32[3,64,4]{2,1,0:T(8,128)S(1)}, u32[]{:S(2)}, u32[]{:S(2)}) collective-permute-start(f32[3,64,4]{2,1,0:T(8,128)S(1)} %get-tuple-element.434), channel_id=1, source_target_pairs={{0,8},{8,16},{16,24},{24,0},{1,9},{9,17},{17,25},{25,1},{2,10},{10... | collective-permute-start | bytes 9224 | tf_op jit(solution)/shard_map/while/body/eval_jaxpr/ppermute | solution.py:23
  587.7 3.6 collective-permute-done
  591.3 3.4 collective-permute-done.1
  595.4 1.5 collective-permute-done.2
  596.9 2.7 collective-permute-done.3
  603.5 0.6 fusion.257
  604.5 0.8 collective-permute-start
  605.4 1.3 collective-permute-start.1
  606.6 3.0 collective-permute-done
  609.6 2.2 collective-permute-done.1
  612.5 1.4 collective-permute-done.2
  613.9 2.5 collective-permute-done.3
  621.9 1.6 collective-permute-start.1
  623.5 2.6 collective-permute-done
  626.1 2.2 collective-permute-done.1
  629.0 1.4 collective-permute-done.2
  630.4 2.5 collective-permute-done.3
  637.9 1.5 collective-permute-start
  640.0 2.6 collective-permute-done
  642.6 3.3 collective-permute-done.1
  646.6 1.4 collective-permute-done.2
  648.0 2.5 collective-permute-done.3
  655.8 0.7 slice_bitcast_fusion.34
  656.6 7.1 %fusion.227 = (f32[2,512,900]{1,2,0:T(8,128)}, f32[2,512,900]{1,2,0:T(8,128)}) fusion(f32[4,512,900]{1,2,0:T(8,128)} %bitcast.40), kind=kLoop, calls=%fused_computation.289 | loop fusion | bytes 14745600 | tf_op jit(solution)/shard_map/slice | solution.py:143
  663.7 4.8 copy.118
  668.5 5.1 copy.119
  673.6 9.0 %fusion.214 = f32[1,2,64,900]{3,0,2,1:T(1,128)S(1)} fusion(f32[2,8,64,900]{3,2,1,0:T(8,128)} %bitcast.264, f32[8]{0:T(128)S(1)} %copy-done.13, f32[]{:T(128)} %reduce_sum.23), kind=kOutput, calls=%fused_computation.265 | convolution fusion | flops 11059208 | bytes 4147236 | tf_op jit(solution)/shard_map/k,ckij->cij/dot_general | solution.py:144
  682.7 2.8 add_multiply_fusion
  (304 shorter events, 30.7 us)
Async XLA Ops:
  9.2 6.5 copy-start.6
  9.2 133.1 %copy-start.12 = (f32[8]{0:T(128)S(1)}, f32[8]{0:T(128)}, u32[]{:S(2)}) copy-start(f32[8]{0:T(128)} %param.10) | copy-start | bytes 100
  9.2 170.4 %all-to-all-start = ((f32[4,512,900]{1,2,0:T(8,128)}), f32[4,512,900]{1,2,0:T(8,128)}, u32[]{:S(2)}, u32[]{:S(2)}) async-start(f32[4,512,900]{1,2,0:T(8,128)} %copy.117), calls=%async_computation | async-start | bytes 14811136 | tf_op jit(solution)/shard_map/all_to_all | solution.py:96
  15.7 120.2 %collective-permute-start.5 = (s32[64,5]{1,0:T(8,128)S(1)}, s32[64,5]{1,0:T(8,128)S(1)}, u32[]{:S(2)}, u32[]{:S(2)}) collective-permute-start(s32[64,5]{1,0:T(8,128)S(1)} %get-tuple-element.324), channel_id=1, source_target_pairs={{8,0},{16,8},{24,16},{0,24},{9,1},{17,9},{25,17},{1,25},{10,2},{18... | collective-permute-start | bytes 3848 | tf_op jit(solution)/shard_map/ppermute | solution.py:24
  19.9 121.3 %collective-permute-start.4 = (s32[64,5]{1,0:T(8,128)S(1)}, s32[64,5]{1,0:T(8,128)S(1)}, u32[]{:S(2)}, u32[]{:S(2)}) collective-permute-start(s32[64,5]{1,0:T(8,128)S(1)} %get-tuple-element.323), channel_id=1, source_target_pairs={{0,8},{8,16},{16,24},{24,0},{1,9},{9,17},{17,25},{25,1},{2,10},{10... | collective-permute-start | bytes 3848 | tf_op jit(solution)/shard_map/ppermute | solution.py:23
  141.3 2.6 collective-permute-start.7
  142.2 4.2 collective-permute-start.6
  147.2 0.7 copy-start.9
  147.2 0.8 copy-start.7
  148.0 37.0 %copy-start.11 = (s32[256]{0:T(256)S(1)}, s32[256]{0:T(256)}, u32[]{:S(2)}) copy-start(s32[256]{0:T(256)} %param.11) | copy-start | bytes 3076
  229.2 13.1 %copy-start.2 = (f32[512,60,60]{0,1,2:T(8,128)}, f32[512,60,60]{0,1,2:T(8,128)S(1)}, u32[]{:S(2)}) copy-start(f32[512,60,60]{0,1,2:T(8,128)S(1)} %get-tuple-element.246) | copy-start | bytes 22118404 | tf_op jit(solution)/shard_map/cond
  263.2 10.0 %copy-start.3 = (f32[512,60,60]{0,1,2:T(8,128)S(1)}, f32[512,60,60]{0,1,2:T(8,128)}, u32[]{:S(2)}) copy-start(f32[512,60,60]{0,1,2:T(8,128)} %copy-done.2) | copy-start | bytes 22118404 | tf_op jit(solution)/shard_map/cond
  306.3 3.1 copy-start.1
  351.3 15.7 %copy-start.5 = (f32[512,60,60]{0,2,1:T(8,128)S(1)}, f32[512,60,60]{0,2,1:T(8,128)}, u32[]{:S(2)}) copy-start(f32[512,60,60]{0,2,1:T(8,128)} %get-tuple-element.243) | copy-start | bytes 22118404 | tf_op jit(solution)/shard_map/cond
  399.8 9.1 %copy-start = (f32[3,64,900]{2,1,0:T(8,128)S(1)}, f32[3,64,900]{2,1,0:T(8,128)}, u32[]{:S(2)}) copy-start(f32[3,64,900]{2,1,0:T(8,128)} %param.12) | copy-start | bytes 2073604
  399.8 256.8 %all-to-all-start.1 = ((f32[512,4,900]{0,2,1:T(8,128)}), f32[512,4,900]{0,2,1:T(8,128)}, u32[]{:S(2)}, u32[]{:S(2)}) async-start(f32[512,4,900]{0,2,1:T(8,128)} %all_to_all.33), calls=%async_computation.1 | async-start | bytes 14811136 | tf_op jit(solution)/shard_map/all_to_all | solution.py:107
  408.9 246.7 %copy-start.8 = (f32[74,910]{1,0:T(8,128)S(1)}, f32[74,910]{1,0:T(8,128)}, u32[]{:S(2)}) copy-start(f32[74,910]{1,0:T(8,128)} %copy-done.7) | copy-start | bytes 808084
  408.9 246.7 %copy-start.10 = (f32[74,910]{1,0:T(8,128)S(1)}, f32[74,910]{1,0:T(8,128)}, u32[]{:S(2)}) copy-start(f32[74,910]{1,0:T(8,128)} %copy-done.9) | copy-start | bytes 808084
  408.9 120.7 %collective-permute-start = (f32[3,64,4]{2,1,0:T(8,128)S(1)}, f32[3,64,4]{2,1,0:T(8,128)S(1)}, u32[]{:S(2)}, u32[]{:S(2)}) collective-permute-start(f32[3,64,4]{2,1,0:T(8,128)S(1)} %get-tuple-element.433), channel_id=1, source_target_pairs={{8,0},{16,8},{24,16},{0,24},{9,1},{17,9},{25,17},{1,25},{10,2},{18... | collective-permute-start | bytes 9224 | tf_op jit(solution)/shard_map/while/body/eval_jaxpr/ppermute | solution.py:24
  412.8 122.0 %collective-permute-start.1 = (f32[3,64,4]{2,1,0:T(8,128)S(1)}, f32[3,64,4]{2,1,0:T(8,128)S(1)}, u32[]{:S(2)}, u32[]{:S(2)}) collective-permute-start(f32[3,64,4]{2,1,0:T(8,128)S(1)} %get-tuple-element.434), channel_id=1, source_target_pairs={{0,8},{8,16},{16,24},{24,0},{1,9},{9,17},{17,25},{25,1},{2,10},{10... | collective-permute-start | bytes 9224 | tf_op jit(solution)/shard_map/while/body/eval_jaxpr/ppermute | solution.py:23
  534.9 2.0 collective-permute-start.2
  535.2 4.8 collective-permute-start.3
  545.0 46.3 %collective-permute-start = (f32[3,64,4]{2,1,0:T(8,128)S(1)}, f32[3,64,4]{2,1,0:T(8,128)S(1)}, u32[]{:S(2)}, u32[]{:S(2)}) collective-permute-start(f32[3,64,4]{2,1,0:T(8,128)S(1)} %get-tuple-element.433), channel_id=1, source_target_pairs={{8,0},{16,8},{24,16},{0,24},{9,1},{17,9},{25,17},{1,25},{10,2},{18... | collective-permute-start | bytes 9224 | tf_op jit(solution)/shard_map/while/body/eval_jaxpr/ppermute | solution.py:24
  545.0 49.6 %collective-permute-start.1 = (f32[3,64,4]{2,1,0:T(8,128)S(1)}, f32[3,64,4]{2,1,0:T(8,128)S(1)}, u32[]{:S(2)}, u32[]{:S(2)}) collective-permute-start(f32[3,64,4]{2,1,0:T(8,128)S(1)} %get-tuple-element.434), channel_id=1, source_target_pairs={{0,8},{8,16},{16,24},{24,0},{1,9},{9,17},{17,25},{25,1},{2,10},{10... | collective-permute-start | bytes 9224 | tf_op jit(solution)/shard_map/while/body/eval_jaxpr/ppermute | solution.py:23
  594.8 2.1 collective-permute-start.2
  595.1 4.4 collective-permute-start.3
  604.5 5.0 collective-permute-start
  605.4 6.4 collective-permute-start.1
  611.9 2.0 collective-permute-start.2
  612.0 4.5 collective-permute-start.3
  621.4 4.7 collective-permute-start
  621.9 6.4 collective-permute-start.1
  628.4 2.0 collective-permute-start.2
  628.5 4.5 collective-permute-start.3
  637.9 4.7 collective-permute-start
  639.5 6.4 collective-permute-start.1
  646.0 2.0 collective-permute-start.2
  646.1 4.5 collective-permute-start.3
  663.7 9.9 %copy-start.13 = (f32[8]{0:T(128)S(1)}, f32[8]{0:T(128)}, u32[]{:S(2)}) copy-start(f32[8]{0:T(128)} %param.10) | copy-start | bytes 100
  673.5 9.1 %copy-start.4 = (f32[2,512,900]{2,1,0:T(8,128)S(1)}, f32[2,512,900]{2,1,0:T(8,128)}, u32[]{:S(2)}) copy-start(f32[2,512,900]{2,1,0:T(8,128)} %copy.119) | copy-start | bytes 11059204
where the time goes:
time: 693 us; the launch traced here: 686 us
  waiting for transfers between devices  321 us (46%)
  matrix products  191 us (28%)
  starting transfers between devices  76.8 us (11%)
  local copies, waits for them, and re-layouts  72.5 us (10%)
  other arithmetic  20.9 us (3%)
    ppermute x12, waiting for transfers between devices, with_halo(): after = lax.ppermute(initial, axis, down)  252 us
    ppermute x12, starting transfers between devices, with_halo(): before = lax.ppermute(last, axis, up)  48.6 us
    ppermute x12, waiting for transfers between devices, with_halo(): before = lax.ppermute(last, axis, up)  37.3 us
    all_to_all x1, waiting for transfers between devices, body(): lax.all_to_all(flattened, 'lon', split_axis=0, concat_axis=1, tiled=True)  31.4 us
    dot_general x1, matrix products, spectral_cut(): jnp.einsum('imq,qk->imk', spec_real, sin_second, precision=highest)  22 us
    dot_general x1, matrix products, spectral_cut(): jnp.einsum('imb,bk->imk', turn_real, sin_second, precision=highest)  20.5 us
    dot_general x1, matrix products, spectral_cut(): jnp.einsum('imb,bk->imk', turn_real, cos_second, precision=highest)  20 us
    dot_general x1, matrix products, spectral_cut(): step_real = jnp.einsum('inb,nm->imb', grid, cos_first, precision=highest)  19.7 us
  transfers between devices with their start and end apart: 26, of which 25 were waited for; matrix products, arithmetic and copies ran while one was open for 4% of the time, Pallas kernels for 0%

commit v1 on v0

v1 whole, which is shorter than its diff:
```python
import functools
import math

import jax
import jax.numpy as jnp
import numpy as np
from jax import lax
from jax.experimental import pallas as pl
from jax.experimental.pallas import tpu as pltpu
from jax.sharding import PartitionSpec as P

SUB = 20
HALO = -(-(SUB + 2) // 8) * 8
wave_coef = 0.65
RESIDUAL = 3e-8


def two_part(table):
    high = table.astype(jnp.bfloat16)
    low = (table - high.astype(np.float64)).astype(jnp.bfloat16)
    return high, low


def cosecant(circle, cols, shift):
    gap = (np.arange(cols)[None, :] + shift - np.arange(cols)[:, None]).astype(np.float64)
    sine = np.sin(np.pi * gap / circle)
    near = gap == 0
    return np.where(near, 0.0, 1.0 / np.where(near, 1.0, sine)) / circle


def cross_factors(block):
    rest = block.copy()
    left, right = [], []
    while True:
        spot = np.unravel_index(np.argmax(np.abs(rest)), rest.shape)
        pivot = rest[spot]
        if abs(pivot) < RESIDUAL:
            break
        column = rest[:, spot[1]] / math.sqrt(abs(pivot))
        row = rest[spot[0]] * (math.copysign(1.0, pivot) / math.sqrt(abs(pivot)))
        left.append(column)
        right.append(row)
        rest = rest - column[:, None] * row[None, :]
    pad = -len(left) % 8
    zero = [np.zeros(block.shape[0])] * pad
    return np.stack(left + zero), np.stack(right + zero)


@functools.lru_cache(maxsize=None)
def tables(circle, cols):
    devices = circle // cols
    pairs = [cross_factors(cosecant(circle, cols, cols * o)) for o in range(1, devices)]
    ranks = tuple(p[0].shape[0] for p in pairs)
    send = np.concatenate([p[0] for p in pairs])
    take = np.concatenate([p[1] for p in pairs])
    return ranks, two_part(cosecant(circle, cols, 0)), two_part(send), two_part(take)


def split(value):
    high = value.astype(jnp.bfloat16)
    low = (value - high.astype(jnp.float32)).astype(jnp.bfloat16)
    return high, low


def product(a, b, dims):
    def dot(p, q):
        return lax.dot_general(p, q, (dims, ((), ())), preferred_element_type=jnp.float32)

    return dot(a[0], b[0]) + (dot(a[1], b[0]) + dot(a[0], b[1]))


def turned(x, cos, sin):
    levels, rows, cols = x.shape
    both = jnp.concatenate([x * cos[None], x * sin[None]], axis=0)
    return split(both.reshape(2 * levels * rows, cols))


def moment_kernel(ranks, x_ref, cos_ref, sin_ref, high_ref, low_ref, sign_ref, *out_refs):
    wave = turned(x_ref[0], cos_ref[...], sin_ref[...])
    moments = product((high_ref[...], low_ref[...]), wave, ((1,), (1,)))
    moments = moments * sign_ref[:, 0:1]
    start = 0
    for rank, out_ref in zip(ranks, out_refs):
        out_ref[...] = moments[start : start + rank]
        start += rank


def filtered_block(n_far, refs):
    x_ref, cos_ref, sin_ref, diag_ref, near_high, near_low, far_high, far_low = refs[:8]
    x = x_ref[0]
    levels, rows, cols = x.shape
    cos, sin = cos_ref[...], sin_ref[...]
    total = product(turned(x, cos, sin), (near_high[...], near_low[...]), ((1,), (0,)))
    far = jnp.concatenate([r[...] for r in refs[8 : 8 + n_far]], axis=0)
    total = total + product(split(far.T), (far_high[...], far_low[...]), ((1,), (0,)))
    total = total.reshape(2, levels, rows, cols)
    return sin[None] * total[0] - cos[None] * total[1] + diag_ref[:, 0:1][None] * x


def tracer_kernel(n_far, *refs):
    refs[-1][0] = filtered_block(n_far, refs)


def velocity_kernel(n_far, *refs):
    weight_ref, open_ref, flow_ref, out_ref = refs[8 + n_far :]
    value = filtered_block(n_far, refs)
    column = value[0] * weight_ref[0]
    for k in range(1, value.shape[0]):
        column = column + value[k] * weight_ref[k]
    out_ref[0] = open_ref[0][None] * (value - column[None] + flow_ref[0][None])


def subcycle_kernel(rows, cols, pad_ref, level_ref, open_ref, flow_ref, state, opens):
    high, wide = pad_ref.shape[1:]
    ocean = pad_ref[3]
    opens[0] = ocean * wave_coef
    opens[1] = ocean * pltpu.roll(ocean, wide - 1, 1)
    opens[2] = ocean * pltpu.roll(ocean, high - 1, 0)
    state[0] = pad_ref[0]
    state[1] = pad_ref[1] * opens[1]
    state[2] = pad_ref[2] * opens[2]

    def step(i, carry):
        east, north = state[1], state[2]
        div = east - pltpu.roll(east, 1, 1) + north - pltpu.roll(north, 1, 0)
        surface = state[0] - opens[0] * div
        state[0] = surface
        state[1] = opens[1] * (
            east - wave_coef * (pltpu.roll(surface, wide - 1, 1) - surface)
        )
        state[2] = opens[2] * (
            north - wave_coef * (pltpu.roll(surface, high - 1, 0) - surface)
        )
        return carry

    lax.fori_loop(0, SUB, step, 0)
    level_ref[...] = state[0, :rows, :cols]
    open_ref[...] = opens[1:, :rows, :cols]
    flow_ref[...] = state[1:, :rows, :cols]


def shifted(value, axis, offset, ring):
    count = lax.axis_size(axis)
    pairs = [(i, (i + offset) % count) for i in range(count) if ring or 0 <= i + offset < count]
    return lax.ppermute(value, axis, pairs)


def barotropic_steps(barotropic, land_sea):
    rows, cols = land_sea.shape
    own = jnp.concatenate([barotropic, land_sea.astype(jnp.float32)[None]])
    west = shifted(own[:, :, cols - HALO :], "lon", 1, True)
    east = shifted(own[:, :, :HALO], "lon", -1, True)
    gap = -(cols + 2 * HALO) % 128
    wide = jnp.concatenate([own, east, jnp.zeros((4, rows, gap), jnp.float32), west], axis=2)
    south = shifted(wide[:, rows - HALO :], "lat", 1, False)
    north = shifted(wide[:, :HALO], "lat", -1, False)
    padded = jnp.concatenate([wide, north, south], axis=1)
    shape = padded.shape[1:]
    pair = jax.ShapeDtypeStruct((2, rows, cols), jnp.float32)
    return pl.pallas_call(
        functools.partial(subcycle_kernel, rows, cols),
        out_shape=(jax.ShapeDtypeStruct((rows, cols), jnp.float32), pair, pair),
        scratch_shapes=[pltpu.VMEM((3,) + shape, jnp.float32)] * 2,
        cost_estimate=pl.CostEstimate(
            flops=SUB * 100 * shape[0] * shape[1], bytes_accessed=0, transcendentals=0
        ),
        name="subcycles",
    )(padded)


def body(fields, thickness, cutoff, barotropic, land_sea):
    lon_count, lat_count = lax.axis_size("lon"), lax.axis_size("lat")
    lat_index, lon_index = lax.axis_index("lat"), lax.axis_index("lon")
    components, levels, rows, cols = fields.shape
    circle, total_rows = cols * lon_count, rows * lat_count
    ranks, near, send, take = tables(circle, cols)
    n_far = len(ranks)

    pole_rows = cutoff.shape[0] // 2
    row_ids = lat_index * rows + lax.iota(jnp.int32, rows)
    slots = jnp.where(row_ids < pole_rows, row_ids, row_ids - (total_rows - 2 * pole_rows))
    polar = (row_ids < pole_rows) | (row_ids >= total_rows - pole_rows)
    match = slots[:, None] == lax.broadcasted_iota(jnp.int32, (1, 2 * pole_rows), 1)
    cuts = jnp.sum(jnp.where(match, cutoff[None, :], 0), axis=1)
    cut_rows = polar & (2 * cuts < circle)
    odd = jnp.where(cut_rows, 2 * cuts + 1, 0)
    place = lon_index * cols + lax.iota(jnp.int32, cols)
    angle = ((odd[:, None] * place[None, :]) % (2 * circle)).astype(jnp.float32) * (
        math.pi / circle
    )
    cos = jnp.where(cut_rows[:, None], jnp.cos(angle), 0.0)
    sin = jnp.where(cut_rows[:, None], jnp.sin(angle), 0.0)
    diag = jnp.where(cut_rows, odd.astype(jnp.float32) / circle, 1.0)
    diag = jnp.broadcast_to(diag[:, None], (rows, 128))
    offsets = np.repeat(np.arange(1, lon_count), ranks)
    sign = jnp.where(lon_index + offsets >= lon_count, -1.0, 1.0).astype(jnp.float32)
    sign = jnp.broadcast_to(sign[:, None], (sum(ranks), 128))

    take_rows = 32 if rows % 32 == 0 else rows
    steps = rows // take_rows
    items = 2 * levels * take_rows
    part = components // 2

    def whole(array):
        return pl.BlockSpec(array.shape, lambda f, h: (0,) * array.ndim)

    def field_spec(first):
        return pl.BlockSpec((1, levels, take_rows, cols), lambda f, h: (f + first, 0, h, 0))

    row_spec = pl.BlockSpec((take_rows, cols), lambda f, h: (h, 0))
    diag_spec = pl.BlockSpec((take_rows, 128), lambda f, h: (h, 0))
    pair_spec = pl.BlockSpec((1, take_rows, cols), lambda f, h: (f, h, 0))

    def moment_specs(first):
        return [pl.BlockSpec((r, items), lambda f, h: (0, (f + first) * steps + h)) for r in ranks]

    moments = pl.pallas_call(
        functools.partial(moment_kernel, ranks),
        grid=(components, steps),
        in_specs=[field_spec(0), row_spec, row_spec, whole(send[0]), whole(send[1]), whole(sign)],
        out_specs=moment_specs(0),
        out_shape=[
            jax.ShapeDtypeStruct((r, components * steps * items), jnp.float32) for r in ranks
        ],
        cost_estimate=pl.CostEstimate(
            flops=20 * fields.size * 64, bytes_accessed=4 * fields.size, transcendentals=0
        ),
        name="moments",
    )(fields, cos, sin, send[0], send[1], sign)
    far = [shifted(m, "lon", o + 1, True) for o, m in enumerate(moments)]

    sea_level, opens, flows = barotropic_steps(barotropic, land_sea)
    weights = thickness / jnp.sum(thickness)

    def apply(kernel, first, specs, args, name):
        return pl.pallas_call(
            functools.partial(kernel, n_far),
            grid=(part, steps),
            in_specs=[field_spec(first), row_spec, row_spec, diag_spec]
            + [whole(t) for t in near + take]
            + moment_specs(first)
            + specs,
            out_specs=field_spec(0),
            out_shape=jax.ShapeDtypeStruct((part,) + fields.shape[1:], jnp.float32),
            cost_estimate=pl.CostEstimate(
                flops=12 * part * levels * rows * cols * cols,
                bytes_accessed=4 * fields.size,
                transcendentals=0,
            ),
            name=name,
        )(fields, cos, sin, diag, *near, *take, *far, *args)

    tracers = apply(tracer_kernel, 0, [], [], "tracers")
    smem = pl.BlockSpec(memory_space=pltpu.SMEM)
    velocity = apply(
        velocity_kernel, part, [smem, pair_spec, pair_spec], [weights, opens, flows], "velocity"
    )
    return tracers, velocity, sea_level


def solution(mesh):
    return jax.shard_map(
        body,
        mesh=mesh,
        in_specs=(P(None, None, "lat", "lon"), P(), P(), P(None, "lat", "lon"), P("lat", "lon")),
        out_specs=(P(None, None, "lat", "lon"), P(None, None, "lat", "lon"), P("lat", "lon")),
        check_vma=False,
    )
```

time: 693 us -> 101 us (0.15)
  waiting for transfers between devices: 321 us -> 7.59 us
  matrix products: 191 us -> 0 us
  local copies, waits for them, and re-layouts: 72.5 us -> 1.43 us
  Pallas kernels: 0 us -> 68.6 us
  starting transfers between devices: 76.8 us -> 14.3 us
  other arithmetic: 20.9 us -> 7.75 us
    ppermute x24 -> x7, waiting for transfers between devices: 290 us -> 7.59 us  [shifted(): return lax.ppermute(value, axis, pairs)]
    dot_general x13 -> x0, matrix products: 191 us -> none  [the longest x1 22 us: spectral_cut(): jnp.einsum('imq,qk->imk', spec_real, sin_second, precision=highest)]
    pallas_call x0 -> x4, Pallas kernels: none -> 68.6 us  [the longest x2 43.5 us: apply(): pl.pallas_call(functools.partial(kernel, n_far), grid=(part, steps), in_s...]
    ppermute x24 -> x7, starting transfers between devices: 61.2 us -> 14.3 us  [shifted(): return lax.ppermute(value, axis, pairs)]
    all_to_all x2 -> x0, waiting for transfers between devices: 31.4 us -> none  [the longest x1 31.4 us: body(): lax.all_to_all(flattened, 'lon', split_axis=0, concat_axis=1, tiled=True)]
    all_to_all x3 -> x0, local copies, waits for them, and re-layouts: 19.3 us -> none  [the longest x2 13.9 us: body(): lax.all_to_all(flattened, 'lon', split_axis=0, concat_axis=1, tiled=True)]
    slice x17 -> x0, local copies, waits for them, and re-layouts: 17.7 us -> none  [the longest x2 12.2 us: body(): currents = filtered[2:]]
    all_to_all x2 -> x0, starting transfers between devices: 15.6 us -> none  [the longest x1 9.13 us: body(): lax.all_to_all(result, 'lon', split_axis=1, concat_axis=0, tiled=True)]
  transfers between devices with their start and end apart: 26 -> 7, of which waited for: 25 -> 2; matrix products, arithmetic and copies ran while one was open for 4% -> 6% of each run, Pallas kernels for 0% -> 33%
where the time goes in v1:
time: 101 us; the launch traced here: 100 us
  Pallas kernels  68.6 us (68%)
  starting transfers between devices  14.3 us (14%)
  other arithmetic  7.75 us (8%)
  waiting for transfers between devices  7.59 us (8%)
  local copies, waits for them, and re-layouts  1.43 us (1%)
    pallas_call x2, Pallas kernels, apply(): pl.pallas_call(functools.partial(kernel, n_far), grid=(part, steps), in_s...  43.5 us
    ppermute x7, starting transfers between devices, shifted(): return lax.ppermute(value, axis, pairs)  14.3 us
    pallas_call x1, Pallas kernels, barotropic_steps(): pl.pallas_call(functools.partial(subcycle_kernel, rows, cols), out_shape=...  13.7 us
    pallas_call x1, Pallas kernels, body(): pl.pallas_call(functools.partial(moment_kernel, ranks), grid=(components,...  11.4 us
    ppermute x7, waiting for transfers between devices, shifted(): return lax.ppermute(value, axis, pairs)  7.59 us
  transfers between devices with their start and end apart: 7, of which 2 were waited for; matrix products, arithmetic and copies ran while one was open for 6% of the time, Pallas kernels for 33%

profile of v1, /device:TPU:0, one launch (start us, length us, event | category | flops | bytes accessed | tf_op | source)
XLA Modules:
  0.0 100.4 jit_solution(16112349385140276552)
XLA Ops:
  0.6 0.0 copy-start.5
  0.6 0.0 copy-start.1
  0.7 1.0 convert_bitcast_fusion
  1.6 1.1 %pad_maximum_fusion.7 = (f32[4,64,24]{2,1,0:T(8,128)S(1)}, f32[4,64,24]{2,1,0:T(8,128)S(1)}) fusion(f32[1,64,900]{2,1,0:T(8,128)S(1)} %convert_bitcast_fusion, f32[3,64,900]{2,1,0:T(8,128)} %param.15), kind=kLoop, calls=%fused_computation.17 | loop fusion | flops 12288 | bytes 970752 | tf_op jit(solution)/shard_map/slice | solution.py:152
  2.7 5.1 %collective-permute-start.3 = (f32[4,64,24]{2,1,0:T(8,128)S(1)}, f32[4,64,24]{2,1,0:T(8,128)S(1)}, u32[]{:S(2)}, u32[]{:S(2)}) collective-permute-start(f32[4,64,24]{2,1,0:T(8,128)S(1)} %get-tuple-element.19), channel_id=1, source_target_pairs={{0,24},{8,0},{16,8},{24,16},{1,25},{9,1},{17,9},{25,17},{2,26},{10... | collective-permute-start | bytes 73736 | tf_op jit(solution)/shard_map/ppermute | solution.py:145
  7.8 0.0 collective-permute-start.4
  7.8 0.0 copy-done.5
  7.9 0.0 copy-done.1
  7.9 0.2 select_reduce_fusion
  8.1 2.0 %sine_select_fusion = (f32[64,900]{1,0:T(8,128)}, f32[64,900]{1,0:T(8,128)}) fusion(s32[900]{0:T(1024)S(1)} %iota_add_fusion, s32[64]{0:T(128)S(1)} %add_select_fusion.1, pred[64]{0:T(512)(128)(4,1)S(1)} %get-tuple-element.16), kind=kLoop, calls=%fused_computation.10 | loop fusion | flops 633600 | bytes 464720 | tf_op jit(solution)/shard_map/jit(_where)/select_n | solution.py:192
  10.1 0.7 broadcast_in_dim.77.sign_ref
  10.8 0.0 copy-start.4
  10.8 0.0 copy-start
  10.8 11.4 %moments.1 = (f32[16,4096]{1,0:T(8,128)}, f32[8,4096]{1,0:T(8,128)}, f32[16,4096]{1,0:T(8,128)}) custom-call(f32[4,8,64,900]{3,2,1,0:T(8,128)} %refs_0_.3, f32[64,900]{1,0:T(8,128)} %get-tuple-element.22.cos_ref.refs_1_, f32[64,900]{1,0:T(8,128)} %get-tuple-element.21.sin_ref.refs_2_, bf16[40,900]{1,0:T(8,128)(2,1)} %constant.67.clone.high_ref, ...), custom_call_target="tpu_custom_call" | custom-call | flops 2359296000 | bytes 7372800 | tf_op jit(solution)/shard_map/moments/pallas_call | solution.py:217
  22.1 1.0 %collective-permute-start.1 = (f32[8,4096]{1,0:T(8,128)}, f32[8,4096]{1,0:T(8,128)}, u32[]{:S(2)}, u32[]{:S(2)}) collective-permute-start(f32[8,4096]{1,0:T(8,128)} %get-tuple-element.10), channel_id=1, source_target_pairs={{0,16},{8,24},{16,0},{24,8},{1,17},{9,25},{17,1},{25,9},{2,18},{10... | collective-permute-start | bytes 393224 | tf_op jit(solution)/shard_map/ppermute | solution.py:145
  23.2 3.4 %collective-permute-start = (f32[16,4096]{1,0:T(8,128)}, f32[16,4096]{1,0:T(8,128)S(1)}, u32[]{:S(2)}, u32[]{:S(2)}) collective-permute-start(f32[16,4096]{1,0:T(8,128)} %get-tuple-element.9), channel_id=1, source_target_pairs={{0,8},{8,16},{16,24},{24,0},{1,9},{9,17},{17,25},{25,1},{2,10},{10... | collective-permute-start | bytes 786440 | tf_op jit(solution)/shard_map/ppermute | solution.py:145
  26.5 0.5 collective-permute-start.2
  27.0 0.0 copy-done.4
  27.0 0.7 reduce_sum.19
  27.6 1.2 %broadcast_divide_fusion.refs_11_ = f32[8]{0:T(128)} fusion(f32[8]{0:T(128)S(1)} %copy-done.4, f32[]{:T(128)} %reduce_sum.19), kind=kLoop, calls=%fused_computation.28 | loop fusion | flops 8 | bytes 68 | tf_op jit(solution)/shard_map/div | solution.py:233
  28.8 0.0 collective-permute-done.3
  28.8 0.0 collective-permute-done.4
  28.9 0.0 copy-done
  28.9 0.2 pad_maximum_fusion.5
  29.1 1.3 %collective-permute-start.5 = (f32[4,24,1024]{2,1,0:T(8,128)S(1)}, f32[4,24,1024]{2,1,0:T(8,128)S(1)}, u32[]{:S(2)}, u32[]{:S(2)}) collective-permute-start(f32[4,24,1024]{2,1,0:T(8,128)S(1)} %get-tuple-element.17), channel_id=1, source_target_pairs={{1,0},{2,1},{3,2},{4,3},{5,4},{6,5},{7,6},{9,8},{10,9},{11,10},{12... | collective-permute-start | bytes 1179656 | tf_op jit(solution)/shard_map/ppermute | solution.py:145
  30.4 3.1 %collective-permute-start.6 = (f32[4,24,1024]{2,1,0:T(8,128)S(1)}, f32[4,24,1024]{2,1,0:T(8,128)S(1)}, u32[]{:S(2)}, u32[]{:S(2)}) collective-permute-start(f32[4,24,1024]{2,1,0:T(8,128)S(1)} %get-tuple-element.18), channel_id=1, source_target_pairs={{0,1},{1,2},{2,3},{3,4},{4,5},{5,6},{6,7},{8,9},{9,10},{10,11},{11... | collective-permute-start | bytes 1179656 | tf_op jit(solution)/shard_map/ppermute | solution.py:145
  33.4 4.4 %collective-permute-done.1.refs_9_ = f32[8,4096]{1,0:T(8,128)} collective-permute-done((f32[8,4096]{1,0:T(8,128)}, f32[8,4096]{1,0:T(8,128)}, u32[]{:S(2)}, u32[]{:S(2)}) %collective-permute-start.1) | collective-permute-done | bytes 131104 | tf_op jit(solution)/shard_map/ppermute | solution.py:145
  37.8 0.0 collective-permute-done.refs_8_
  37.8 0.0 copy-start.2
  37.8 3.2 %collective-permute-done.2.refs_10_ = f32[16,4096]{1,0:T(8,128)S(1)} collective-permute-done((f32[16,4096]{1,0:T(8,128)}, f32[16,4096]{1,0:T(8,128)S(1)}, u32[]{:S(2)}, u32[]{:S(2)}) %collective-permute-start.2) | collective-permute-done | bytes 262176 | tf_op jit(solution)/shard_map/ppermute | solution.py:145
  41.0 0.0 copy-start.3
  41.0 0.7 broadcast_in_dim.74.refs_3_
  41.7 0.0 copy-done.2
  41.7 0.0 copy-done.3
  41.7 21.4 %tracers.1 = f32[2,8,64,900]{3,2,1,0:T(8,128)} custom-call(f32[4,8,64,900]{3,2,1,0:T(8,128)} %refs_0_.3, f32[64,900]{1,0:T(8,128)} %get-tuple-element.22.cos_ref.refs_1_, f32[64,900]{1,0:T(8,128)} %get-tuple-element.21.sin_ref.refs_2_, f32[64,128]{1,0:T(8,128)} %broadcast_in_dim.74.refs_3_, bf16[900,900]{1,0:T(8,128)(2,1)} %constant.69.clone.refs_4_, ...), custom_call_target="tpu_custom_call" | custom-call | flops 9953280000 | bytes 7372800 | tf_op jit(solution)/shard_map/tracers/pallas_call | solution.py:236
  63.1 0.0 collective-permute-done.5
  63.1 0.0 collective-permute-done.6
  63.1 1.5 %pad_maximum_fusion.pad_ref = f32[4,112,1024]{2,1,0:T(8,128)} fusion(f32[4,24,1024]{2,1,0:T(8,128)S(1)} %collective-permute-done.6, f32[4,24,1024]{2,1,0:T(8,128)S(1)} %collective-permute-done.5, f32[4,64,24]{2,1,0:T(8,128)S(1)} %collective-permute-done.4, f32[4,64,76]{2,1,0:T(8,128)S(1)} %broadcast_in_dim.79, f32[4,64,24]{2,1,0:T(8,128)S(1)} %collective-permute-done.3, ...), kind=kLoop, calls=%fused_computation | loop fusion | flops 2752512 | bytes 3670016 | tf_op jit(solution)/shard_map/concatenate | solution.py:157
  64.6 13.7 %subcycles.1 = (f32[64,900]{1,0:T(8,128)}, f32[2,64,900]{2,1,0:T(8,128)}, f32[2,64,900]{2,1,0:T(8,128)}) custom-call(f32[4,112,1024]{2,1,0:T(8,128)} %pad_maximum_fusion.pad_ref), custom_call_target="tpu_custom_call" | custom-call | flops 229376000 | tf_op jit(solution)/shard_map/subcycles/pallas_call | solution.py:160
  78.3 22.1 %velocity.1 = f32[2,8,64,900]{3,2,1,0:T(8,128)} custom-call(f32[4,8,64,900]{3,2,1,0:T(8,128)} %refs_0_.3, f32[64,900]{1,0:T(8,128)} %get-tuple-element.22.cos_ref.refs_1_, f32[64,900]{1,0:T(8,128)} %get-tuple-element.21.sin_ref.refs_2_, f32[64,128]{1,0:T(8,128)} %broadcast_in_dim.74.refs_3_, bf16[900,900]{1,0:T(8,128)(2,1)} %constant.69.clone.refs_4_, ...), custom_call_target="tpu_custom_call" | custom-call | flops 9953280000 | bytes 7372800 | tf_op jit(solution)/shard_map/velocity/pallas_call | solution.py:236
  (6 shorter events, 0.0 us)
Async XLA Ops:
  0.6 7.2 %copy-start.5 = (s32[40]{0:T(128)S(1)}, s32[40]{0:T(128)}, u32[]{:S(2)}) copy-start(s32[40]{0:T(128)} %constant.66.clone) | copy-start | bytes 484
  0.6 7.2 %copy-start.1 = (s32[256]{0:T(256)S(1)}, s32[256]{0:T(256)}, u32[]{:S(2)}) copy-start(s32[256]{0:T(256)} %param.14) | copy-start | bytes 3076
  2.7 26.1 %collective-permute-start.3 = (f32[4,64,24]{2,1,0:T(8,128)S(1)}, f32[4,64,24]{2,1,0:T(8,128)S(1)}, u32[]{:S(2)}, u32[]{:S(2)}) collective-permute-start(f32[4,64,24]{2,1,0:T(8,128)S(1)} %get-tuple-element.19), channel_id=1, source_target_pairs={{0,24},{8,0},{16,8},{24,16},{1,25},{9,1},{17,9},{25,17},{2,26},{10... | collective-permute-start | bytes 73736 | tf_op jit(solution)/shard_map/ppermute | solution.py:145
  7.8 21.0 %collective-permute-start.4 = (f32[4,64,24]{2,1,0:T(8,128)S(1)}, f32[4,64,24]{2,1,0:T(8,128)S(1)}, u32[]{:S(2)}, u32[]{:S(2)}) collective-permute-start(f32[4,64,24]{2,1,0:T(8,128)S(1)} %get-tuple-element.20), channel_id=1, source_target_pairs={{0,8},{8,16},{16,24},{24,0},{1,9},{9,17},{17,25},{25,1},{2,10},{10... | collective-permute-start | bytes 73736 | tf_op jit(solution)/shard_map/ppermute | solution.py:145
  10.8 16.2 %copy-start.4 = (f32[8]{0:T(128)S(1)}, f32[8]{0:T(128)}, u32[]{:S(2)}) copy-start(f32[8]{0:T(128)} %param.13) | copy-start | bytes 100
  10.8 18.1 %copy-start = (f32[3,64,900]{2,1,0:T(8,128)S(1)}, f32[3,64,900]{2,1,0:T(8,128)}, u32[]{:S(2)}) copy-start(f32[3,64,900]{2,1,0:T(8,128)} %param.15) | copy-start | bytes 2073604
  22.1 15.6 %collective-permute-start.1 = (f32[8,4096]{1,0:T(8,128)}, f32[8,4096]{1,0:T(8,128)}, u32[]{:S(2)}, u32[]{:S(2)}) collective-permute-start(f32[8,4096]{1,0:T(8,128)} %get-tuple-element.10), channel_id=1, source_target_pairs={{0,16},{8,24},{16,0},{24,8},{1,17},{9,25},{17,1},{25,9},{2,18},{10... | collective-permute-start | bytes 393224 | tf_op jit(solution)/shard_map/ppermute | solution.py:145
  23.2 14.6 %collective-permute-start = (f32[16,4096]{1,0:T(8,128)}, f32[16,4096]{1,0:T(8,128)S(1)}, u32[]{:S(2)}, u32[]{:S(2)}) collective-permute-start(f32[16,4096]{1,0:T(8,128)} %get-tuple-element.9), channel_id=1, source_target_pairs={{0,8},{8,16},{16,24},{24,0},{1,9},{9,17},{17,25},{25,1},{2,10},{10... | collective-permute-start | bytes 786440 | tf_op jit(solution)/shard_map/ppermute | solution.py:145
  26.5 14.5 %collective-permute-start.2 = (f32[16,4096]{1,0:T(8,128)}, f32[16,4096]{1,0:T(8,128)S(1)}, u32[]{:S(2)}, u32[]{:S(2)}) collective-permute-start(f32[16,4096]{1,0:T(8,128)} %get-tuple-element.11), channel_id=1, source_target_pairs={{0,24},{8,0},{16,8},{24,16},{1,25},{9,1},{17,9},{25,17},{2,26},{10... | collective-permute-start | bytes 786440 | tf_op jit(solution)/shard_map/ppermute | solution.py:145
  29.1 34.0 %collective-permute-start.5 = (f32[4,24,1024]{2,1,0:T(8,128)S(1)}, f32[4,24,1024]{2,1,0:T(8,128)S(1)}, u32[]{:S(2)}, u32[]{:S(2)}) collective-permute-start(f32[4,24,1024]{2,1,0:T(8,128)S(1)} %get-tuple-element.17), channel_id=1, source_target_pairs={{1,0},{2,1},{3,2},{4,3},{5,4},{6,5},{7,6},{9,8},{10,9},{11,10},{12... | collective-permute-start | bytes 1179656 | tf_op jit(solution)/shard_map/ppermute | solution.py:145
  30.4 32.7 %collective-permute-start.6 = (f32[4,24,1024]{2,1,0:T(8,128)S(1)}, f32[4,24,1024]{2,1,0:T(8,128)S(1)}, u32[]{:S(2)}, u32[]{:S(2)}) collective-permute-start(f32[4,24,1024]{2,1,0:T(8,128)S(1)} %get-tuple-element.18), channel_id=1, source_target_pairs={{0,1},{1,2},{2,3},{3,4},{4,5},{5,6},{6,7},{8,9},{9,10},{10,11},{11... | collective-permute-start | bytes 1179656 | tf_op jit(solution)/shard_map/ppermute | solution.py:145
  37.8 3.9 %copy-start.2 = (f32[16,4096]{1,0:T(8,128)}, f32[16,4096]{1,0:T(8,128)S(1)}, u32[]{:S(2)}) copy-start(f32[16,4096]{1,0:T(8,128)S(1)} %collective-permute-done.refs_8_) | copy-start | bytes 786436
  41.0 0.7 copy-start.3

commit v2 on v1

v2 whole, which is shorter than its diff:
```python
import functools
import math

import jax
import jax.numpy as jnp
import numpy as np
from jax import lax
from jax.experimental import pallas as pl
from jax.experimental.pallas import tpu as pltpu
from jax.sharding import PartitionSpec as P

SUB = 20
HALO = -(-(SUB + 2) // 8) * 8
wave_coef = 0.65
RESIDUAL = 3e-8


def two_part(table):
    high = table.astype(jnp.bfloat16)
    low = (table - high.astype(np.float64)).astype(jnp.bfloat16)
    return high, low


def cosecant(circle, cols, shift):
    gap = (np.arange(cols)[None, :] + shift - np.arange(cols)[:, None]).astype(np.float64)
    sine = np.sin(np.pi * gap / circle)
    near = gap == 0
    return np.where(near, 0.0, 1.0 / np.where(near, 1.0, sine)) / circle


def cross_factors(block):
    rest = block.copy()
    left, right = [], []
    while True:
        spot = np.unravel_index(np.argmax(np.abs(rest)), rest.shape)
        pivot = rest[spot]
        if abs(pivot) < RESIDUAL:
            break
        column = rest[:, spot[1]] / math.sqrt(abs(pivot))
        row = rest[spot[0]] * (math.copysign(1.0, pivot) / math.sqrt(abs(pivot)))
        left.append(column)
        right.append(row)
        rest = rest - column[:, None] * row[None, :]
    pad = -len(left) % 8
    rows, cols = block.shape
    return np.stack(left + [np.zeros(rows)] * pad), np.stack(right + [np.zeros(cols)] * pad)


@functools.lru_cache(maxsize=None)
def tables(circle, cols):
    devices = circle // cols
    cut = -(-cols // 512) * 256
    near = cosecant(circle, cols, 0)
    pairs = [cross_factors(cosecant(circle, cols, cols * o)) for o in range(1, devices)]
    for source, target in ((slice(0, cut), slice(cut, cols)), (slice(cut, cols), slice(0, cut))):
        part = cross_factors(near[source, target])
        whole = [np.zeros((part[0].shape[0], cols)) for _ in range(2)]
        whole[0][:, source], whole[1][:, target] = part
        pairs.append(tuple(whole))
    ranks = tuple(p[0].shape[0] for p in pairs)
    ranks = ranks[: devices - 1] + (sum(ranks[devices - 1 :]),)
    send = two_part(np.concatenate([p[0] for p in pairs]).T)
    width = -(-sum(ranks) // 128) * 128
    room = ((0, 0), (0, width - sum(ranks)))
    send = np.concatenate([np.pad(part, room) for part in send], axis=1)
    take = two_part(np.concatenate([p[1] for p in pairs]))
    take = np.concatenate([take[0], take[0], take[1]])
    side = max(cut, cols - cut)
    return cut, ranks, two_part(near[:side, :side]), send, take


def split(value):
    high = value.astype(jnp.bfloat16)
    low = (value - high.astype(jnp.float32)).astype(jnp.bfloat16)
    return high, low


def dot(a, b):
    return lax.dot_general(a, b, (((1,), (0,)), ((), ())), preferred_element_type=jnp.float32)


def turned(x, cos, sin):
    levels, rows, cols = x.shape
    both = jnp.concatenate([x * cos[None], x * sin[None]], axis=0)
    return split(both.reshape(2 * levels * rows, cols))


def moment_kernel(ranks, x_ref, cos_ref, sin_ref, send_ref, *out_refs):
    cols = x_ref.shape[-1]
    high, low = turned(x_ref[0], cos_ref[:, :cols], sin_ref[...])
    width = send_ref.shape[1] // 2
    both = dot(high, send_ref[...])
    moments = both[:, :width] + (both[:, width:] + dot(low, send_ref[:, :width]))
    moments = moments.T
    count, place = lax.axis_size("lon"), lax.axis_index("lon")
    start = 0
    for offset, (rank, out_ref) in enumerate(zip(ranks, out_refs), 1):
        group = moments[start : start + rank]
        if offset < count:
            group = group * jnp.where(place + offset >= count, -1.0, 1.0)
        out_ref[...] = group
        start += rank


def filtered_block(cut, n_far, refs):
    x_ref, cos_ref, sin_ref, near_high, near_low, take_ref = refs[:6]
    x = x_ref[0]
    levels, rows, cols = x.shape
    cos, sin = cos_ref[:, :cols], sin_ref[...]
    diag = cos_ref[:, cols : cols + 1]
    high, low = turned(x, cos, sin)
    far = jnp.concatenate([r[...] for r in refs[6 : 6 + n_far]], axis=0)
    far_high = far.astype(jnp.bfloat16).astype(jnp.float32)
    far = jnp.concatenate([far_high, far - far_high, far_high], axis=0).T.astype(jnp.bfloat16)
    outs = []
    for a, b in ((0, cut), (cut, cols)):
        n = b - a
        k_high, k_low = near_high[:n, :n], near_low[:n, :n]
        part = dot(high[:, a:b], k_high) + (dot(low[:, a:b], k_high) + dot(high[:, a:b], k_low))
        part = (part + dot(far, take_ref[:, a:b])).reshape(2, levels, rows, n)
        outs.append(
            sin[None, :, a:b] * part[0] - cos[None, :, a:b] * part[1] + diag[None] * x[:, :, a:b]
        )
    return outs


def tracer_kernel(cut, n_far, *refs):
    first, second = filtered_block(cut, n_far, refs)
    refs[-1][0, :, :, :cut] = first
    refs[-1][0, :, :, cut:] = second


def velocity_kernel(cut, n_far, *refs):
    thick_ref, open_ref, flow_ref, out_ref = refs[6 + n_far :]
    first, second = filtered_block(cut, n_far, refs)
    cols = out_ref.shape[-1]
    for value, a, b in ((first, 0, cut), (second, cut, cols)):
        column = value[0] * thick_ref[0]
        depth = thick_ref[0]
        for k in range(1, value.shape[0]):
            column = column + value[k] * thick_ref[k]
            depth = depth + thick_ref[k]
        extra = flow_ref[0, :, a:b] - column / jnp.full(column.shape, depth)
        out_ref[0, :, :, a:b] = open_ref[0, :, a:b][None] * (value + extra[None])


def subcycle_kernel(rows, cols, pad_ref, level_ref, open_ref, flow_ref, state, opens):
    high, wide = pad_ref.shape[1:]
    ocean = pad_ref[3]
    opens[0] = ocean * wave_coef
    opens[1] = ocean * pltpu.roll(ocean, wide - 1, 1)
    opens[2] = ocean * pltpu.roll(ocean, high - 1, 0)
    state[0] = pad_ref[0]
    state[1] = pad_ref[1] * opens[1]
    state[2] = pad_ref[2] * opens[2]

    def step(i, carry):
        east, north = state[1], state[2]
        div = east - pltpu.roll(east, 1, 1) + north - pltpu.roll(north, 1, 0)
        surface = state[0] - opens[0] * div
        state[0] = surface
        state[1] = opens[1] * (
            east - wave_coef * (pltpu.roll(surface, wide - 1, 1) - surface)
        )
        state[2] = opens[2] * (
            north - wave_coef * (pltpu.roll(surface, high - 1, 0) - surface)
        )
        return carry

    lax.fori_loop(0, SUB, step, 0)
    level_ref[...] = state[0, :rows, :cols]
    open_ref[...] = opens[1:, :rows, :cols]
    flow_ref[...] = state[1:, :rows, :cols]


def shifted(value, axis, offset, ring):
    count = lax.axis_size(axis)
    pairs = [(i, (i + offset) % count) for i in range(count) if ring or 0 <= i + offset < count]
    return lax.ppermute(value, axis, pairs)


def tall_tile(barotropic, land_sea):
    rows, cols = land_sea.shape
    own = jnp.concatenate([barotropic, land_sea.astype(jnp.float32)[None]])
    west = shifted(own[:, :, cols - HALO :], "lon", 1, True)
    east = shifted(own[:, :, :HALO], "lon", -1, True)
    gap = -(cols + 2 * HALO) % 128
    wide = jnp.concatenate([own, east, jnp.zeros((4, rows, gap), jnp.float32), west], axis=2)
    last, first = wide[:, rows - HALO :], wide[:, :HALO]
    south = shifted(last, "lat", 1, False)
    north = shifted(first, "lat", -1, False)
    return (last, first), jnp.concatenate([wide, north, south], axis=1)


def barotropic_steps(padded, rows, cols):
    shape = padded.shape[1:]
    pair = jax.ShapeDtypeStruct((2, rows, cols), jnp.float32)
    return pl.pallas_call(
        functools.partial(subcycle_kernel, rows, cols),
        out_shape=(jax.ShapeDtypeStruct((rows, cols), jnp.float32), pair, pair),
        scratch_shapes=[pltpu.VMEM((3,) + shape, jnp.float32)] * 2,
        cost_estimate=pl.CostEstimate(
            flops=SUB * 1000 * shape[0] * shape[1], bytes_accessed=0, transcendentals=0
        ),
        name="subcycles",
    )(padded)


def body(fields, thickness, cutoff, barotropic, land_sea):
    lon_count, lat_count = lax.axis_size("lon"), lax.axis_size("lat")
    lat_index, lon_index = lax.axis_index("lat"), lax.axis_index("lon")
    components, levels, rows, cols = fields.shape
    circle, total_rows = cols * lon_count, rows * lat_count
    cut, ranks, near, send, take = tables(circle, cols)
    n_far = len(ranks)

    pole_rows = cutoff.shape[0] // 2
    row_ids = lat_index * rows + lax.iota(jnp.int32, rows)
    slots = jnp.where(row_ids < pole_rows, row_ids, row_ids - (total_rows - 2 * pole_rows))
    polar = (row_ids < pole_rows) | (row_ids >= total_rows - pole_rows)
    match = slots[:, None] == lax.broadcasted_iota(jnp.int32, (1, 2 * pole_rows), 1)
    cuts = jnp.sum(jnp.where(match, cutoff[None, :], 0), axis=1)
    cut_rows = polar & (2 * cuts < circle)
    odd = jnp.where(cut_rows, 2 * cuts + 1, 0)
    room = (cols // 128 + 1) * 128
    place = lon_index * cols + lax.iota(jnp.int32, room)
    angle = ((odd[:, None] * place[None, :]) % (2 * circle)).astype(jnp.float32) * (
        math.pi / circle
    )
    cos = jnp.where(cut_rows[:, None], jnp.cos(angle), 0.0)
    sin = jnp.where(cut_rows[:, None], jnp.sin(angle), 0.0)[:, :cols]
    diag = jnp.where(cut_rows, odd.astype(jnp.float32) / circle, 1.0)
    cos = jnp.where(lax.iota(jnp.int32, room)[None] < cols, cos, diag[:, None])

    take_rows = 32 if rows % 32 == 0 else rows
    steps = rows // take_rows
    items = 2 * levels * take_rows
    part = components // 2

    def whole(array):
        return pl.BlockSpec(array.shape, lambda f, h: (0,) * array.ndim)

    def field_spec(first):
        return pl.BlockSpec((1, levels, take_rows, cols), lambda f, h: (f + first, 0, h, 0))

    row_spec = pl.BlockSpec((take_rows, cols), lambda f, h: (h, 0))
    wide_spec = pl.BlockSpec((take_rows, room), lambda f, h: (h, 0))
    pair_spec = pl.BlockSpec((1, take_rows, cols), lambda f, h: (f, h, 0))

    def moment_specs(first):
        return [pl.BlockSpec((r, items), lambda f, h: (0, (f + first) * steps + h)) for r in ranks]

    edges, padded = tall_tile(barotropic, land_sea)
    cos, sin, _ = lax.optimization_barrier((cos, sin, edges))
    moments = pl.pallas_call(
        functools.partial(moment_kernel, ranks),
        grid=(components, steps),
        in_specs=[field_spec(0), wide_spec, row_spec, whole(send)],
        out_specs=moment_specs(0),
        out_shape=[
            jax.ShapeDtypeStruct((r, components * steps * items), jnp.float32) for r in ranks
        ],
        cost_estimate=pl.CostEstimate(
            flops=20 * fields.size * 64, bytes_accessed=4 * fields.size, transcendentals=0
        ),
        name="moments",
    )(fields, cos, sin, send)
    far = [shifted(m, "lon", o + 1, True) for o, m in enumerate(moments[:-1])]
    sea_level, opens, flows = barotropic_steps(padded, rows, cols)
    far, opens, flows = lax.optimization_barrier((far, opens, flows))
    far = far + [moments[-1]]

    def apply(kernel, first, specs, args, name):
        return pl.pallas_call(
            functools.partial(kernel, cut, n_far),
            grid=(part, steps),
            in_specs=[field_spec(first), wide_spec, row_spec]
            + [whole(t) for t in near + (take,)]
            + moment_specs(first)
            + specs,
            out_specs=field_spec(0),
            out_shape=jax.ShapeDtypeStruct((part,) + fields.shape[1:], jnp.float32),
            cost_estimate=pl.CostEstimate(
                flops=12 * part * levels * rows * cols * cols,
                bytes_accessed=4 * fields.size,
                transcendentals=0,
            ),
            name=name,
        )(fields, cos, sin, *near, take, *far, *args)

    tracers = apply(tracer_kernel, 0, [], [], "tracers")
    smem = pl.BlockSpec(memory_space=pltpu.SMEM)
    velocity = apply(
        velocity_kernel, part, [smem, pair_spec, pair_spec], [thickness, opens, flows], "velocity"
    )
    return tracers, velocity, sea_level


def solution(mesh):
    return jax.shard_map(
        body,
        mesh=mesh,
        in_specs=(P(None, None, "lat", "lon"), P(), P(), P(None, "lat", "lon"), P("lat", "lon")),
        out_specs=(P(None, None, "lat", "lon"), P(None, None, "lat", "lon"), P("lat", "lon")),
        check_vma=False,
    )
```

time: 101 us -> 76.4 us (0.76)
  Pallas kernels: 68.6 us -> 48.6 us
  waiting for transfers between devices: 7.59 us -> 4.73 us
    pallas_call x2, Pallas kernels: 43.5 us -> 24.6 us  [apply(): pl.pallas_call(functools.partial(kernel, cut, n_far), grid=(part, steps),...]
    ppermute x7, waiting for transfers between devices: 7.59 us -> 4.73 us  [shifted(): return lax.ppermute(value, axis, pairs)]
    mul x0 -> x1, other arithmetic: none -> 1.8 us  [body(): (odd[:, None] * place[None, :] % (2 * circle)).astype(jnp.float32)]
    broadcast_in_dim x3 -> x1, local copies, waits for them, and re-layouts: 1.38 us -> 0.01 us  [tall_tile(): jnp.zeros((4, rows, gap), jnp.float32)]
    div x1 -> x0, other arithmetic: 1.19 us -> none  [body(): weights = thickness / jnp.sum(thickness)]
    pallas_call x1, Pallas kernels: 11.4 us -> 10.2 us  [body(): pl.pallas_call(functools.partial(moment_kernel, ranks), grid=(components,...]
  transfers between devices with their start and end apart: 7 -> 7, of which waited for: 2 -> 2; matrix products, arithmetic and copies ran while one was open for 6% -> 7% of each run, Pallas kernels for 33% -> 32%
where the time goes in v2:
time: 76.4 us; the launch traced here: 75.9 us
  Pallas kernels  48.6 us (64%)
  starting transfers between devices  13.7 us (18%)
  other arithmetic  7.35 us (10%)
  waiting for transfers between devices  4.73 us (6%)
  local copies, waits for them, and re-layouts  0.8 us (1%)
    pallas_call x2, Pallas kernels, apply(): pl.pallas_call(functools.partial(kernel, cut, n_far), grid=(part, steps),...  24.6 us
    pallas_call x1, Pallas kernels, barotropic_steps(): pl.pallas_call(functools.partial(subcycle_kernel, rows, cols), out_shape=...  13.8 us
    ppermute x7, starting transfers between devices, shifted(): return lax.ppermute(value, axis, pairs)  13.7 us
    pallas_call x1, Pallas kernels, body(): pl.pallas_call(functools.partial(moment_kernel, ranks), grid=(components,...  10.2 us
    ppermute x7, waiting for transfers between devices, shifted(): return lax.ppermute(value, axis, pairs)  4.73 us
    mul x1, other arithmetic, body(): (odd[:, None] * place[None, :] % (2 * circle)).astype(jnp.float32)  1.8 us
    select_n x1, other arithmetic, body(): sin = jnp.where(cut_rows[:, None], jnp.sin(angle), 0.0)[:, :cols]  1.58 us
  transfers between devices with their start and end apart: 7, of which 2 were waited for; matrix products, arithmetic and copies ran while one was open for 7% of the time, Pallas kernels for 32%

profile of v2, /device:TPU:0, one launch (start us, length us, event | category | flops | bytes accessed | tf_op | source)
XLA Modules:
  0.0 75.9 jit_solution(3941568598146855557)
XLA Ops:
  0.6 0.0 copy-start
  0.6 0.0 copy-start.1
  0.7 1.0 %convert_bitcast_fusion = f32[1,64,900]{2,1,0:T(8,128)S(1)} fusion(s32[64,900]{1,0:T(8,128)} %param.13), kind=kLoop, calls=%fused_computation.11 | loop fusion | flops 57600 | bytes 460800 | tf_op jit(solution)/shard_map/broadcast_in_dim | solution.py:184
  1.7 1.1 %pad_maximum_fusion.7 = (f32[4,64,24]{2,1,0:T(8,128)S(1)}, f32[4,64,24]{2,1,0:T(8,128)S(1)}) fusion(f32[1,64,900]{2,1,0:T(8,128)S(1)} %convert_bitcast_fusion, f32[3,64,900]{2,1,0:T(8,128)} %param.12), kind=kLoop, calls=%fused_computation.18 | loop fusion | flops 12288 | bytes 970752 | tf_op jit(solution)/shard_map/slice | solution.py:186
  2.8 5.1 %collective-permute-start = (f32[4,64,24]{2,1,0:T(8,128)S(1)}, f32[4,64,24]{2,1,0:T(8,128)S(1)}, u32[]{:S(2)}, u32[]{:S(2)}) collective-permute-start(f32[4,64,24]{2,1,0:T(8,128)S(1)} %get-tuple-element.35), channel_id=1, source_target_pairs={{0,24},{8,0},{16,8},{24,16},{1,25},{9,1},{17,9},{25,17},{2,26},{10... | collective-permute-start | bytes 73736 | tf_op jit(solution)/shard_map/ppermute | solution.py:179
  7.9 0.0 collective-permute-start.1
  7.9 0.0 copy-done.1
  7.9 0.2 select_reduce_fusion
  8.2 1.8 %fusion.1 = (f32[64,1024]{1,0:T(8,128)S(1)}, f32[64,1024]{1,0:T(8,128)}) fusion(s32[1024]{0:T(1024)S(1)} %iota_add_fusion, s32[64]{0:T(128)S(1)} %get-tuple-element.31, f32[64]{0:T(128)S(1)} %multiply_select_fusion, pred[64]{0:T(512)(128)(4,1)S(1)} %get-tuple-element.32, pred[1024]{0:T(1024)(128)(4,1)S(1)} %iota_compare_fusion.1), kind=kLoop, calls=%fused_computation.8 | loop fusion | flops 720896 | bytes 529984 | tf_op jit(solution)/shard_map/mul | solution.py:227
  10.0 1.8 %collective-permute-done = f32[4,64,24]{2,1,0:T(8,128)S(1)} collective-permute-done((f32[4,64,24]{2,1,0:T(8,128)S(1)}, f32[4,64,24]{2,1,0:T(8,128)S(1)}, u32[]{:S(2)}, u32[]{:S(2)}) %collective-permute-start) | collective-permute-done | bytes 24608 | tf_op jit(solution)/shard_map/ppermute | solution.py:179
  11.8 2.9 %collective-permute-done.1 = f32[4,64,24]{2,1,0:T(8,128)S(1)} collective-permute-done((f32[4,64,24]{2,1,0:T(8,128)S(1)}, f32[4,64,24]{2,1,0:T(8,128)S(1)}, u32[]{:S(2)}, u32[]{:S(2)}) %collective-permute-start.1) | collective-permute-done | bytes 24608 | tf_op jit(solution)/shard_map/ppermute | solution.py:179
  14.7 0.0 copy-done
  14.7 0.2 pad_maximum_fusion.1
  14.9 1.3 %collective-permute-start.5 = (f32[4,24,1024]{2,1,0:T(8,128)S(1)}, f32[4,24,1024]{2,1,0:T(8,128)S(1)}, u32[]{:S(2)}, u32[]{:S(2)}) collective-permute-start(f32[4,24,1024]{2,1,0:T(8,128)S(1)} %get-tuple-element.33), channel_id=1, source_target_pairs={{1,0},{2,1},{3,2},{4,3},{5,4},{6,5},{7,6},{9,8},{10,9},{11,10},{12... | collective-permute-start | bytes 1179656 | tf_op jit(solution)/shard_map/ppermute | solution.py:179
  16.2 3.1 %collective-permute-start.6 = (f32[4,24,1024]{2,1,0:T(8,128)S(1)}, f32[4,24,1024]{2,1,0:T(8,128)S(1)}, u32[]{:S(2)}, u32[]{:S(2)}) collective-permute-start(f32[4,24,1024]{2,1,0:T(8,128)S(1)} %get-tuple-element.34), channel_id=1, source_target_pairs={{0,1},{1,2},{2,3},{3,4},{4,5},{5,6},{6,7},{8,9},{9,10},{10,11},{11... | collective-permute-start | bytes 1179656 | tf_op jit(solution)/shard_map/ppermute | solution.py:179
  19.2 1.6 %fusion.2.sin_ref.refs_2_ = f32[64,900]{1,0:T(8,128)} fusion(f32[64,1024]{1,0:T(8,128)S(1)} %get-tuple-element.37, pred[64]{0:T(512)(128)(4,1)S(1)} %get-tuple-element.32), kind=kLoop, calls=%fused_computation.10 | loop fusion | flops 57600 | bytes 460864 | tf_op jit(solution)/shard_map/jit(_where)/select_n | solution.py:231
  20.8 10.2 %moments.1 = (f32[16,4096]{1,0:T(8,128)}, f32[8,4096]{1,0:T(8,128)}, f32[16,4096]{1,0:T(8,128)}, f32[32,4096]{1,0:T(8,128)}) custom-call(f32[4,8,64,900]{3,2,1,0:T(8,128)} %refs_0_.3, f32[64,1024]{1,0:T(8,128)} %get-tuple-element.17.cos_ref.refs_1_, f32[64,900]{1,0:T(8,128)} %fusion.2.sin_ref.refs_2_, bf16[900,256]{1,0:T(8,128)(2,1)} %constant.57.clone.send_ref), custom_call_target="tpu_custom_call" | custom-call | flops 2359296000 | bytes 7372800 | tf_op jit(solution)/shard_map/moments/pallas_call | solution.py:255
  31.0 0.4 collective-permute-start.3
  31.5 1.6 %collective-permute-start.2 = (f32[16,4096]{1,0:T(8,128)}, f32[16,4096]{1,0:T(8,128)S(1)}, u32[]{:S(2)}, u32[]{:S(2)}) collective-permute-start(f32[16,4096]{1,0:T(8,128)} %get-tuple-element.19), channel_id=1, source_target_pairs={{0,8},{8,16},{16,24},{24,0},{1,9},{9,17},{17,25},{25,1},{2,10},{10... | collective-permute-start | bytes 786440 | tf_op jit(solution)/shard_map/ppermute | solution.py:179
  33.1 2.2 %collective-permute-start.4 = (f32[16,4096]{1,0:T(8,128)}, f32[16,4096]{1,0:T(8,128)S(1)}, u32[]{:S(2)}, u32[]{:S(2)}) collective-permute-start(f32[16,4096]{1,0:T(8,128)} %get-tuple-element.21), channel_id=1, source_target_pairs={{0,24},{8,0},{16,8},{24,16},{1,25},{9,1},{17,9},{25,17},{2,26},{10... | collective-permute-start | bytes 786440 | tf_op jit(solution)/shard_map/ppermute | solution.py:179
  35.3 0.0 collective-permute-done.5
  35.3 0.0 collective-permute-done.6
  35.3 1.5 %pad_maximum_fusion.pad_ref = f32[4,112,1024]{2,1,0:T(8,128)} fusion(f32[4,24,1024]{2,1,0:T(8,128)S(1)} %collective-permute-done.6, f32[4,24,1024]{2,1,0:T(8,128)S(1)} %collective-permute-done.5, f32[4,64,24]{2,1,0:T(8,128)S(1)} %collective-permute-done.1, f32[4,64,76]{2,1,0:T(8,128)S(1)} %broadcast_in_dim.75, f32[4,64,24]{2,1,0:T(8,128)S(1)} %collective-permute-done, ...), kind=kLoop, calls=%fused_computation | loop fusion | flops 2752512 | bytes 3670016 | tf_op jit(solution)/shard_map/concatenate | solution.py:192
  36.8 13.8 %subcycles.1 = (f32[64,900]{1,0:T(8,128)}, f32[2,64,900]{2,1,0:T(8,128)}, f32[2,64,900]{2,1,0:T(8,128)}) custom-call(f32[4,112,1024]{2,1,0:T(8,128)} %pad_maximum_fusion.pad_ref), custom_call_target="tpu_custom_call" | custom-call | flops 2293760000 | tf_op jit(solution)/shard_map/subcycles/pallas_call | solution.py:198
  50.5 0.0 collective-permute-done.3.refs_7_
  50.5 0.0 collective-permute-done.2.refs_6_
  50.5 0.0 copy-start.2
  50.6 0.0 collective-permute-done.4.refs_8_
  50.6 0.0 copy-start.3
  50.6 0.7 copy-done.2
  51.3 0.1 copy-done.3
  51.3 11.9 %tracers.1 = f32[2,8,64,900]{3,2,1,0:T(8,128)} custom-call(f32[4,8,64,900]{3,2,1,0:T(8,128)} %refs_0_.3, f32[64,1024]{1,0:T(8,128)} %get-tuple-element.17.cos_ref.refs_1_, f32[64,900]{1,0:T(8,128)} %fusion.2.sin_ref.refs_2_, bf16[512,512]{1,0:T(8,128)(2,1)} %constant.58.clone.refs_3_, bf16[512,512]{1,0:T(8,128)(2,1)} %constant.59.clone.refs_4_, ...), custom_call_target="tpu_custom_call" | custom-call | flops 9953280000 | bytes 7372800 | tf_op jit(solution)/shard_map/tracers/pallas_call | solution.py:274
  63.3 12.7 %velocity.1 = f32[2,8,64,900]{3,2,1,0:T(8,128)} custom-call(f32[4,8,64,900]{3,2,1,0:T(8,128)} %refs_0_.3, f32[64,1024]{1,0:T(8,128)} %get-tuple-element.17.cos_ref.refs_1_, f32[64,900]{1,0:T(8,128)} %fusion.2.sin_ref.refs_2_, bf16[512,512]{1,0:T(8,128)(2,1)} %constant.58.clone.refs_3_, bf16[512,512]{1,0:T(8,128)(2,1)} %constant.59.clone.refs_4_, ...), custom_call_target="tpu_custom_call" | custom-call | flops 9953280000 | bytes 7372800 | tf_op jit(solution)/shard_map/velocity/pallas_call | solution.py:274
  (6 shorter events, 0.0 us)
Async XLA Ops:
  0.6 14.1 %copy-start = (f32[3,64,900]{2,1,0:T(8,128)S(1)}, f32[3,64,900]{2,1,0:T(8,128)}, u32[]{:S(2)}) copy-start(f32[3,64,900]{2,1,0:T(8,128)} %param.12) | copy-start | bytes 2073604
  0.6 7.3 %copy-start.1 = (s32[256]{0:T(256)S(1)}, s32[256]{0:T(256)}, u32[]{:S(2)}) copy-start(s32[256]{0:T(256)} %param.11) | copy-start | bytes 3076
  2.8 9.0 %collective-permute-start = (f32[4,64,24]{2,1,0:T(8,128)S(1)}, f32[4,64,24]{2,1,0:T(8,128)S(1)}, u32[]{:S(2)}, u32[]{:S(2)}) collective-permute-start(f32[4,64,24]{2,1,0:T(8,128)S(1)} %get-tuple-element.35), channel_id=1, source_target_pairs={{0,24},{8,0},{16,8},{24,16},{1,25},{9,1},{17,9},{25,17},{2,26},{10... | collective-permute-start | bytes 73736 | tf_op jit(solution)/shard_map/ppermute | solution.py:179
  7.9 6.8 %collective-permute-start.1 = (f32[4,64,24]{2,1,0:T(8,128)S(1)}, f32[4,64,24]{2,1,0:T(8,128)S(1)}, u32[]{:S(2)}, u32[]{:S(2)}) collective-permute-start(f32[4,64,24]{2,1,0:T(8,128)S(1)} %get-tuple-element.36), channel_id=1, source_target_pairs={{0,8},{8,16},{16,24},{24,0},{1,9},{9,17},{17,25},{25,1},{2,10},{10... | collective-permute-start | bytes 73736 | tf_op jit(solution)/shard_map/ppermute | solution.py:179
  14.9 20.4 %collective-permute-start.5 = (f32[4,24,1024]{2,1,0:T(8,128)S(1)}, f32[4,24,1024]{2,1,0:T(8,128)S(1)}, u32[]{:S(2)}, u32[]{:S(2)}) collective-permute-start(f32[4,24,1024]{2,1,0:T(8,128)S(1)} %get-tuple-element.33), channel_id=1, source_target_pairs={{1,0},{2,1},{3,2},{4,3},{5,4},{6,5},{7,6},{9,8},{10,9},{11,10},{12... | collective-permute-start | bytes 1179656 | tf_op jit(solution)/shard_map/ppermute | solution.py:179
  16.2 19.1 %collective-permute-start.6 = (f32[4,24,1024]{2,1,0:T(8,128)S(1)}, f32[4,24,1024]{2,1,0:T(8,128)S(1)}, u32[]{:S(2)}, u32[]{:S(2)}) collective-permute-start(f32[4,24,1024]{2,1,0:T(8,128)S(1)} %get-tuple-element.34), channel_id=1, source_target_pairs={{0,1},{1,2},{2,3},{3,4},{4,5},{5,6},{6,7},{8,9},{9,10},{10,11},{11... | collective-permute-start | bytes 1179656 | tf_op jit(solution)/shard_map/ppermute | solution.py:179
  31.0 19.5 %collective-permute-start.3 = (f32[8,4096]{1,0:T(8,128)}, f32[8,4096]{1,0:T(8,128)}, u32[]{:S(2)}, u32[]{:S(2)}) collective-permute-start(f32[8,4096]{1,0:T(8,128)} %get-tuple-element.20), channel_id=1, source_target_pairs={{0,16},{8,24},{16,0},{24,8},{1,17},{9,25},{17,1},{25,9},{2,18},{10... | collective-permute-start | bytes 393224 | tf_op jit(solution)/shard_map/ppermute | solution.py:179
  31.5 19.1 %collective-permute-start.2 = (f32[16,4096]{1,0:T(8,128)}, f32[16,4096]{1,0:T(8,128)S(1)}, u32[]{:S(2)}, u32[]{:S(2)}) collective-permute-start(f32[16,4096]{1,0:T(8,128)} %get-tuple-element.19), channel_id=1, source_target_pairs={{0,8},{8,16},{16,24},{24,0},{1,9},{9,17},{17,25},{25,1},{2,10},{10... | collective-permute-start | bytes 786440 | tf_op jit(solution)/shard_map/ppermute | solution.py:179
  33.1 17.5 %collective-permute-start.4 = (f32[16,4096]{1,0:T(8,128)}, f32[16,4096]{1,0:T(8,128)S(1)}, u32[]{:S(2)}, u32[]{:S(2)}) collective-permute-start(f32[16,4096]{1,0:T(8,128)} %get-tuple-element.21), channel_id=1, source_target_pairs={{0,24},{8,0},{16,8},{24,16},{1,25},{9,1},{17,9},{25,17},{2,26},{10... | collective-permute-start | bytes 786440 | tf_op jit(solution)/shard_map/ppermute | solution.py:179
  50.5 0.7 copy-start.2
  50.6 0.8 %copy-start.3 = (f32[16,4096]{1,0:T(8,128)}, f32[16,4096]{1,0:T(8,128)S(1)}, u32[]{:S(2)}) copy-start(f32[16,4096]{1,0:T(8,128)S(1)} %collective-permute-done.4.refs_8_) | copy-start | bytes 786436

commit v3 on v2

--- a/solution.py
+++ b/solution.py
@@ -87,7 +87,7 @@
 
 def moment_kernel(ranks, x_ref, cos_ref, sin_ref, send_ref, *out_refs):
     cols = x_ref.shape[-1]
-    high, low = turned(x_ref[0], cos_ref[:, :cols], sin_ref[...])
+    high, low = turned(x_ref[0], cos_ref[:, :cols], sin_ref[:, :cols])
     width = send_ref.shape[1] // 2
     both = dot(high, send_ref[...])
     moments = both[:, :width] + (both[:, width:] + dot(low, send_ref[:, :width]))
@@ -106,7 +106,7 @@
     x_ref, cos_ref, sin_ref, near_high, near_low, take_ref = refs[:6]
     x = x_ref[0]
     levels, rows, cols = x.shape
-    cos, sin = cos_ref[:, :cols], sin_ref[...]
+    cos, sin = cos_ref[:, :cols], sin_ref[:, :cols]
     diag = cos_ref[:, cols : cols + 1]
     high, low = turned(x, cos, sin)
     far = jnp.concatenate([r[...] for r in refs[6 : 6 + n_far]], axis=0)
@@ -228,7 +228,7 @@
         math.pi / circle
     )
     cos = jnp.where(cut_rows[:, None], jnp.cos(angle), 0.0)
-    sin = jnp.where(cut_rows[:, None], jnp.sin(angle), 0.0)[:, :cols]
+    sin = jnp.sin(angle)
     diag = jnp.where(cut_rows, odd.astype(jnp.float32) / circle, 1.0)
     cos = jnp.where(lax.iota(jnp.int32, room)[None] < cols, cos, diag[:, None])
 
@@ -243,7 +243,6 @@
     def field_spec(first):
         return pl.BlockSpec((1, levels, take_rows, cols), lambda f, h: (f + first, 0, h, 0))
 
-    row_spec = pl.BlockSpec((take_rows, cols), lambda f, h: (h, 0))
     wide_spec = pl.BlockSpec((take_rows, room), lambda f, h: (h, 0))
     pair_spec = pl.BlockSpec((1, take_rows, cols), lambda f, h: (f, h, 0))
 
@@ -255,7 +254,7 @@
     moments = pl.pallas_call(
         functools.partial(moment_kernel, ranks),
         grid=(components, steps),
-        in_specs=[field_spec(0), wide_spec, row_spec, whole(send)],
+        in_specs=[field_spec(0), wide_spec, wide_spec, whole(send)],
         out_specs=moment_specs(0),
         out_shape=[
             jax.ShapeDtypeStruct((r, components * steps * items), jnp.float32) for r in ranks
@@ -274,7 +273,7 @@
         return pl.pallas_call(
             functools.partial(kernel, cut, n_far),
             grid=(part, steps),
-            in_specs=[field_spec(first), wide_spec, row_spec]
+            in_specs=[field_spec(first), wide_spec, wide_spec]
             + [whole(t) for t in near + (take,)]
             + moment_specs(first)
             + specs,

time: 76.4 us -> 76.8 us (level)
  waiting for transfers between devices: 4.73 us -> 6.53 us
  other arithmetic: 7.35 us -> 5.98 us
    sin x0 -> x1, other arithmetic: none -> 2.01 us  [body(): sin = jnp.sin(angle)]
    mul x1 -> x0, other arithmetic: 1.8 us -> none  [body(): (odd[:, None] * place[None, :] % (2 * circle)).astype(jnp.float32)]
    ppermute x7, waiting for transfers between devices: 4.73 us -> 6.53 us  [shifted(): return lax.ppermute(value, axis, pairs)]
    select_n x1 -> x0, other arithmetic: 1.58 us -> none  [body(): sin = jnp.where(cut_rows[:, None], jnp.sin(angle), 0.0)[:, :cols]]
  transfers between devices with their start and end apart: 7 -> 7, of which waited for: 2 -> 2; matrix products, arithmetic and copies ran while one was open for 7% -> 5% of each run, Pallas kernels for 32% -> 31%
where the time goes in v3:
time: 76.8 us; the launch traced here: 76.4 us
  Pallas kernels  48.6 us (63%)
  starting transfers between devices  13.7 us (18%)
  waiting for transfers between devices  6.53 us (9%)
  other arithmetic  5.98 us (8%)
  local copies, waits for them, and re-layouts  0.8 us (1%)
    pallas_call x2, Pallas kernels, apply(): pl.pallas_call(functools.partial(kernel, cut, n_far), grid=(part, steps),...  24.6 us
    pallas_call x1, Pallas kernels, barotropic_steps(): pl.pallas_call(functools.partial(subcycle_kernel, rows, cols), out_shape=...  13.8 us
    ppermute x7, starting transfers between devices, shifted(): return lax.ppermute(value, axis, pairs)  13.7 us
    pallas_call x1, Pallas kernels, body(): pl.pallas_call(functools.partial(moment_kernel, ranks), grid=(components,...  10.2 us
    ppermute x7, waiting for transfers between devices, shifted(): return lax.ppermute(value, axis, pairs)  6.53 us
    sin x1, other arithmetic, body(): sin = jnp.sin(angle)  2.01 us
  transfers between devices with their start and end apart: 7, of which 2 were waited for; matrix products, arithmetic and copies ran while one was open for 5% of the time, Pallas kernels for 31%

profile of v3, /device:TPU:0, one launch (start us, length us, event | category | flops | bytes accessed | tf_op | source)
XLA Modules:
  0.0 76.4 jit_solution(8270331017693533496)
XLA Ops:
  0.6 0.0 copy-start
  0.6 0.0 copy-start.1
  0.7 1.0 %convert_bitcast_fusion = f32[1,64,900]{2,1,0:T(8,128)S(1)} fusion(s32[64,900]{1,0:T(8,128)} %param.13), kind=kLoop, calls=%fused_computation.9 | loop fusion | flops 57600 | bytes 460800 | tf_op jit(solution)/shard_map/broadcast_in_dim | solution.py:184
  1.7 1.1 %pad_maximum_fusion.7 = (f32[4,64,24]{2,1,0:T(8,128)S(1)}, f32[4,64,24]{2,1,0:T(8,128)S(1)}) fusion(f32[1,64,900]{2,1,0:T(8,128)S(1)} %convert_bitcast_fusion, f32[3,64,900]{2,1,0:T(8,128)} %param.12), kind=kLoop, calls=%fused_computation.17 | loop fusion | flops 12288 | bytes 970752 | tf_op jit(solution)/shard_map/slice | solution.py:186
  2.8 5.1 %collective-permute-start = (f32[4,64,24]{2,1,0:T(8,128)S(1)}, f32[4,64,24]{2,1,0:T(8,128)S(1)}, u32[]{:S(2)}, u32[]{:S(2)}) collective-permute-start(f32[4,64,24]{2,1,0:T(8,128)S(1)} %get-tuple-element.35), channel_id=1, source_target_pairs={{0,24},{8,0},{16,8},{24,16},{1,25},{9,1},{17,9},{25,17},{2,26},{10... | collective-permute-start | bytes 73736 | tf_op jit(solution)/shard_map/ppermute | solution.py:179
  7.9 0.0 collective-permute-start.1
  7.9 0.0 copy-done.1
  7.9 0.2 select_reduce_fusion
  8.2 3.6 %collective-permute-done = f32[4,64,24]{2,1,0:T(8,128)S(1)} collective-permute-done((f32[4,64,24]{2,1,0:T(8,128)S(1)}, f32[4,64,24]{2,1,0:T(8,128)S(1)}, u32[]{:S(2)}, u32[]{:S(2)}) %collective-permute-start) | collective-permute-done | bytes 24608 | tf_op jit(solution)/shard_map/ppermute | solution.py:179
  11.8 2.9 %collective-permute-done.1 = f32[4,64,24]{2,1,0:T(8,128)S(1)} collective-permute-done((f32[4,64,24]{2,1,0:T(8,128)S(1)}, f32[4,64,24]{2,1,0:T(8,128)S(1)}, u32[]{:S(2)}, u32[]{:S(2)}) %collective-permute-start.1) | collective-permute-done | bytes 24608 | tf_op jit(solution)/shard_map/ppermute | solution.py:179
  14.7 0.0 copy-done
  14.7 0.2 pad_maximum_fusion.1
  14.9 1.3 %collective-permute-start.5 = (f32[4,24,1024]{2,1,0:T(8,128)S(1)}, f32[4,24,1024]{2,1,0:T(8,128)S(1)}, u32[]{:S(2)}, u32[]{:S(2)}) collective-permute-start(f32[4,24,1024]{2,1,0:T(8,128)S(1)} %get-tuple-element.33), channel_id=1, source_target_pairs={{1,0},{2,1},{3,2},{4,3},{5,4},{6,5},{7,6},{9,8},{10,9},{11,10},{12... | collective-permute-start | bytes 1179656 | tf_op jit(solution)/shard_map/ppermute | solution.py:179
  16.2 3.1 %collective-permute-start.6 = (f32[4,24,1024]{2,1,0:T(8,128)S(1)}, f32[4,24,1024]{2,1,0:T(8,128)S(1)}, u32[]{:S(2)}, u32[]{:S(2)}) collective-permute-start(f32[4,24,1024]{2,1,0:T(8,128)S(1)} %get-tuple-element.34), channel_id=1, source_target_pairs={{0,1},{1,2},{2,3},{3,4},{4,5},{5,6},{6,7},{8,9},{9,10},{10,11},{11... | collective-permute-start | bytes 1179656 | tf_op jit(solution)/shard_map/ppermute | solution.py:179
  19.2 2.0 %fusion.4 = (f32[64,1024]{1,0:T(8,128)}, f32[64,1024]{1,0:T(8,128)}) fusion(s32[1024]{0:T(1024)S(1)} %iota_add_fusion, s32[64]{0:T(128)S(1)} %get-tuple-element.31, f32[64]{0:T(128)S(1)} %multiply_select_fusion, pred[64]{0:T(512)(128)(4,1)S(1)} %get-tuple-element.32, pred[1024]{0:T(1024)(128)(4,1)S(1)} %iota_compare_fusion.1), kind=kLoop, calls=%fused_computation.14 | loop fusion | flops 720896 | bytes 529984 | tf_op jit(solution)/shard_map/sin | solution.py:231
  21.3 10.2 %moments.1 = (f32[16,4096]{1,0:T(8,128)}, f32[8,4096]{1,0:T(8,128)}, f32[16,4096]{1,0:T(8,128)}, f32[32,4096]{1,0:T(8,128)}) custom-call(f32[4,8,64,900]{3,2,1,0:T(8,128)} %refs_0_.3, f32[64,1024]{1,0:T(8,128)} %get-tuple-element.17.cos_ref.refs_1_, f32[64,1024]{1,0:T(8,128)} %get-tuple-element.18.sin_ref.refs_2_, bf16[900,256]{1,0:T(8,128)(2,1)} %constant.57.clone.send_ref), custom_call_target="tpu_custom_call" | custom-call | flops 2359296000 | bytes 7372800 | tf_op jit(solution)/shard_map/moments/pallas_call | solution.py:254
  31.5 0.4 collective-permute-start.3
  31.9 1.6 %collective-permute-start.2 = (f32[16,4096]{1,0:T(8,128)}, f32[16,4096]{1,0:T(8,128)S(1)}, u32[]{:S(2)}, u32[]{:S(2)}) collective-permute-start(f32[16,4096]{1,0:T(8,128)} %get-tuple-element.19), channel_id=1, source_target_pairs={{0,8},{8,16},{16,24},{24,0},{1,9},{9,17},{17,25},{25,1},{2,10},{10... | collective-permute-start | bytes 786440 | tf_op jit(solution)/shard_map/ppermute | solution.py:179
  33.5 2.2 %collective-permute-start.4 = (f32[16,4096]{1,0:T(8,128)}, f32[16,4096]{1,0:T(8,128)S(1)}, u32[]{:S(2)}, u32[]{:S(2)}) collective-permute-start(f32[16,4096]{1,0:T(8,128)} %get-tuple-element.21), channel_id=1, source_target_pairs={{0,24},{8,0},{16,8},{24,16},{1,25},{9,1},{17,9},{25,17},{2,26},{10... | collective-permute-start | bytes 786440 | tf_op jit(solution)/shard_map/ppermute | solution.py:179
  35.7 0.0 collective-permute-done.5
  35.7 0.0 collective-permute-done.6
  35.7 1.5 %pad_maximum_fusion.pad_ref = f32[4,112,1024]{2,1,0:T(8,128)} fusion(f32[4,24,1024]{2,1,0:T(8,128)S(1)} %collective-permute-done.6, f32[4,24,1024]{2,1,0:T(8,128)S(1)} %collective-permute-done.5, f32[4,64,24]{2,1,0:T(8,128)S(1)} %collective-permute-done.1, f32[4,64,76]{2,1,0:T(8,128)S(1)} %broadcast_in_dim.70, f32[4,64,24]{2,1,0:T(8,128)S(1)} %collective-permute-done, ...), kind=kLoop, calls=%fused_computation | loop fusion | flops 2752512 | bytes 3670016 | tf_op jit(solution)/shard_map/concatenate | solution.py:192
  37.2 13.8 %subcycles.1 = (f32[64,900]{1,0:T(8,128)}, f32[2,64,900]{2,1,0:T(8,128)}, f32[2,64,900]{2,1,0:T(8,128)}) custom-call(f32[4,112,1024]{2,1,0:T(8,128)} %pad_maximum_fusion.pad_ref), custom_call_target="tpu_custom_call" | custom-call | flops 2293760000 | tf_op jit(solution)/shard_map/subcycles/pallas_call | solution.py:198
  51.0 0.0 collective-permute-done.3.refs_7_
  51.0 0.0 collective-permute-done.2.refs_6_
  51.0 0.0 copy-start.2
  51.0 0.0 collective-permute-done.4.refs_8_
  51.0 0.0 copy-start.3
  51.0 0.7 copy-done.2
  51.7 0.1 copy-done.3
  51.8 11.9 %tracers.1 = f32[2,8,64,900]{3,2,1,0:T(8,128)} custom-call(f32[4,8,64,900]{3,2,1,0:T(8,128)} %refs_0_.3, f32[64,1024]{1,0:T(8,128)} %get-tuple-element.17.cos_ref.refs_1_, f32[64,1024]{1,0:T(8,128)} %get-tuple-element.18.sin_ref.refs_2_, bf16[512,512]{1,0:T(8,128)(2,1)} %constant.58.clone.refs_3_, bf16[512,512]{1,0:T(8,128)(2,1)} %constant.59.clone.refs_4_, ...), custom_call_target="tpu_custom_call" | custom-call | flops 9953280000 | bytes 7372800 | tf_op jit(solution)/shard_map/tracers/pallas_call | solution.py:273
  63.7 12.6 %velocity.1 = f32[2,8,64,900]{3,2,1,0:T(8,128)} custom-call(f32[4,8,64,900]{3,2,1,0:T(8,128)} %refs_0_.3, f32[64,1024]{1,0:T(8,128)} %get-tuple-element.17.cos_ref.refs_1_, f32[64,1024]{1,0:T(8,128)} %get-tuple-element.18.sin_ref.refs_2_, bf16[512,512]{1,0:T(8,128)(2,1)} %constant.58.clone.refs_3_, bf16[512,512]{1,0:T(8,128)(2,1)} %constant.59.clone.refs_4_, ...), custom_call_target="tpu_custom_call" | custom-call | flops 9953280000 | bytes 7372800 | tf_op jit(solution)/shard_map/velocity/pallas_call | solution.py:273
  (6 shorter events, 0.0 us)
Async XLA Ops:
  0.6 14.1 %copy-start = (f32[3,64,900]{2,1,0:T(8,128)S(1)}, f32[3,64,900]{2,1,0:T(8,128)}, u32[]{:S(2)}) copy-start(f32[3,64,900]{2,1,0:T(8,128)} %param.12) | copy-start | bytes 2073604
  0.6 7.3 %copy-start.1 = (s32[256]{0:T(256)S(1)}, s32[256]{0:T(256)}, u32[]{:S(2)}) copy-start(s32[256]{0:T(256)} %param.11) | copy-start | bytes 3076
  2.8 9.0 %collective-permute-start = (f32[4,64,24]{2,1,0:T(8,128)S(1)}, f32[4,64,24]{2,1,0:T(8,128)S(1)}, u32[]{:S(2)}, u32[]{:S(2)}) collective-permute-start(f32[4,64,24]{2,1,0:T(8,128)S(1)} %get-tuple-element.35), channel_id=1, source_target_pairs={{0,24},{8,0},{16,8},{24,16},{1,25},{9,1},{17,9},{25,17},{2,26},{10... | collective-permute-start | bytes 73736 | tf_op jit(solution)/shard_map/ppermute | solution.py:179
  7.9 6.8 %collective-permute-start.1 = (f32[4,64,24]{2,1,0:T(8,128)S(1)}, f32[4,64,24]{2,1,0:T(8,128)S(1)}, u32[]{:S(2)}, u32[]{:S(2)}) collective-permute-start(f32[4,64,24]{2,1,0:T(8,128)S(1)} %get-tuple-element.36), channel_id=1, source_target_pairs={{0,8},{8,16},{16,24},{24,0},{1,9},{9,17},{17,25},{25,1},{2,10},{10... | collective-permute-start | bytes 73736 | tf_op jit(solution)/shard_map/ppermute | solution.py:179
  14.9 20.8 %collective-permute-start.5 = (f32[4,24,1024]{2,1,0:T(8,128)S(1)}, f32[4,24,1024]{2,1,0:T(8,128)S(1)}, u32[]{:S(2)}, u32[]{:S(2)}) collective-permute-start(f32[4,24,1024]{2,1,0:T(8,128)S(1)} %get-tuple-element.33), channel_id=1, source_target_pairs={{1,0},{2,1},{3,2},{4,3},{5,4},{6,5},{7,6},{9,8},{10,9},{11,10},{12... | collective-permute-start | bytes 1179656 | tf_op jit(solution)/shard_map/ppermute | solution.py:179
  16.2 19.6 %collective-permute-start.6 = (f32[4,24,1024]{2,1,0:T(8,128)S(1)}, f32[4,24,1024]{2,1,0:T(8,128)S(1)}, u32[]{:S(2)}, u32[]{:S(2)}) collective-permute-start(f32[4,24,1024]{2,1,0:T(8,128)S(1)} %get-tuple-element.34), channel_id=1, source_target_pairs={{0,1},{1,2},{2,3},{3,4},{4,5},{5,6},{6,7},{8,9},{9,10},{10,11},{11... | collective-permute-start | bytes 1179656 | tf_op jit(solution)/shard_map/ppermute | solution.py:179
  31.5 19.5 %collective-permute-start.3 = (f32[8,4096]{1,0:T(8,128)}, f32[8,4096]{1,0:T(8,128)}, u32[]{:S(2)}, u32[]{:S(2)}) collective-permute-start(f32[8,4096]{1,0:T(8,128)} %get-tuple-element.20), channel_id=1, source_target_pairs={{0,16},{8,24},{16,0},{24,8},{1,17},{9,25},{17,1},{25,9},{2,18},{10... | collective-permute-start | bytes 393224 | tf_op jit(solution)/shard_map/ppermute | solution.py:179
  31.9 19.1 %collective-permute-start.2 = (f32[16,4096]{1,0:T(8,128)}, f32[16,4096]{1,0:T(8,128)S(1)}, u32[]{:S(2)}, u32[]{:S(2)}) collective-permute-start(f32[16,4096]{1,0:T(8,128)} %get-tuple-element.19), channel_id=1, source_target_pairs={{0,8},{8,16},{16,24},{24,0},{1,9},{9,17},{17,25},{25,1},{2,10},{10... | collective-permute-start | bytes 786440 | tf_op jit(solution)/shard_map/ppermute | solution.py:179
  33.5 17.5 %collective-permute-start.4 = (f32[16,4096]{1,0:T(8,128)}, f32[16,4096]{1,0:T(8,128)S(1)}, u32[]{:S(2)}, u32[]{:S(2)}) collective-permute-start(f32[16,4096]{1,0:T(8,128)} %get-tuple-element.21), channel_id=1, source_target_pairs={{0,24},{8,0},{16,8},{24,16},{1,25},{9,1},{17,9},{25,17},{2,26},{10... | collective-permute-start | bytes 786440 | tf_op jit(solution)/shard_map/ppermute | solution.py:179
  51.0 0.7 copy-start.2
  51.0 0.8 %copy-start.3 = (f32[16,4096]{1,0:T(8,128)}, f32[16,4096]{1,0:T(8,128)S(1)}, u32[]{:S(2)}) copy-start(f32[16,4096]{1,0:T(8,128)S(1)} %collective-permute-done.4.refs_8_) | copy-start | bytes 786436
